TPU v7x, 32 devices: a whole 2x2x4 slice. The times are simulated.
32 devices in a mesh: grp: 4 (over y, core), dev: 8 (over z, x).
Axes of the slice: x: 2, y: 2, z: 4, core: 2. Of those that a mesh axis runs over, the one named last changes fastest.
Arguments:
- interior_stiffness: float32 [64, 8, 128, 128], P(('grp', 'dev')), may hold values from -6 to 8, as said below
- interior_links: float32 [64, 7, 128, 128], P(('grp', 'dev')), may hold values from -4 to 4
- coupling_stiffness: float32 [64, 128, 256], P(('grp', 'dev')), may hold values from -0.5 to 0.5
- interface_stiffness: float32 [64, 256, 256], P(('grp', 'dev')), may hold values from -5 to 5, as said below
- interior_mass: float32 [64, 1024], P(('grp', 'dev')), may hold values from 0.03 to 0.5
- interface_mass: float32 [64, 256], P(('grp', 'dev')), may hold values from 0.5 to 4
- interior_modes: float32 [64, 1024, 256], P(('grp', 'dev')), may hold values from -6 to 6
- interior_blocks: int32 [64], P(('grp', 'dev')), may hold values from 2 to 8
- interface_blocks: int32 [64, 2], P(('grp', 'dev')), may hold values from 0 to 7, as said below
- parent_modes: float32 [1024, 256], P(('grp', 'dev')), may hold values from -2 to 2
Outputs:
- parent_stiffness: float32 [1024, 1024], P(('grp', 'dev'))
- parent_mass: float32 [1024, 1024], P(('grp', 'dev'))
- coupling: float32 [64, 256, 256], P(('grp', 'dev'))
- modal_stiffness: float32 [256, 256], replicated
- modal_mass: float32 [256, 256], replicated
Inputs may be any that keep to these rules, and one draw needn't show every extreme that they name: `interior_stiffness`: each diagonal block is symmetric; with interior_links, the leading k blocks of every component's block-tridiagonal interior stiffness form a symmetric positive definite matrix for every k from 1 to 8. `interface_stiffness`: Symmetric. `interface_blocks`: the 2 parent blocks of one component are distinct.
All inputs are finite; a program needn't handle non-finite values.
Results may differ from a plain program's by a relative error of at most 0.0003.
Values sent between devices are 32-bit elements; how exact they have to be, the bound alone decides.
No kernel may reach another device: no remote copies, remote signals or barrier semaphores. Data moves between devices by JAX's collectives and lax.ppermute only.
A program may use at most 64 MiB of HBM per device.

v0:
```python
import jax
import jax.numpy as jnp
from jax import lax
from jax.sharding import PartitionSpec as P

BLOCK = 128
NBB = 2
PB = 8


def product(left, right):
    return jnp.dot(left, right, precision=lax.Precision.HIGHEST, preferred_element_type=jnp.float32)


def eliminate_padded(diag_blocks, link_blocks, live_count):
    blocks_total = diag_blocks.shape[0]
    block_width = diag_blocks.shape[1]
    identity = jnp.eye(block_width, dtype=jnp.float32)
    positions = lax.iota(jnp.int32, blocks_total)
    diag_live = jnp.where((positions < live_count)[:, None, None], diag_blocks, identity)
    links_live = jnp.where(
        (positions[1:] < live_count)[:, None, None], link_blocks, jnp.zeros_like(link_blocks)
    )
    coupled_in = jnp.concatenate(
        [jnp.zeros((1, block_width, block_width), jnp.float32), links_live], 0
    )

    def eliminate_advance(previous, pair):
        block_diag, block_low = pair
        crossing = lax.linalg.triangular_solve(
            previous, block_low, left_side=False, lower=True, transpose_a=True
        )
        schur_part = block_diag - product(crossing, crossing.T)
        factor = jnp.linalg.cholesky(schur_part)
        return (factor, (factor, crossing))

    _, (factors, crossings) = lax.scan(eliminate_advance, identity, (diag_live, coupled_in))
    return (factors, crossings)


def solve_padded(factors, crossings, coupled_stiff, live_count):
    blocks_total = factors.shape[0]
    block_width = factors.shape[1]
    last_block = live_count - 1
    end_factor = lax.dynamic_index_in_dim(factors, last_block, 0, keepdims=False)
    forward = lax.linalg.triangular_solve(end_factor, coupled_stiff, left_side=True, lower=True)
    ahead_links = jnp.concatenate(
        [crossings[1:], jnp.zeros((1, block_width, block_width), jnp.float32)], 0
    )
    positions = lax.iota(jnp.int32, blocks_total)

    def solve_advance(following, triple):
        factor, cross_next, position = triple
        source = jnp.where(position == last_block, forward, jnp.zeros_like(forward))
        right_side = source - product(cross_next.T, following)
        solved = lax.linalg.triangular_solve(
            factor, right_side, left_side=True, lower=True, transpose_a=True
        )
        return (solved, solved)

    _, solved = lax.scan(
        solve_advance, jnp.zeros_like(forward), (factors, ahead_links, positions), reverse=True
    )
    return -solved


def project_component(
    constraint, coupled_stiff, edge_stiff, inner_mass, edge_mass, inner_modes, live_count
):
    blocks_total = constraint.shape[0]
    block_width = constraint.shape[1]
    end_rows = lax.dynamic_index_in_dim(constraint, live_count - 1, 0, keepdims=False)
    reduced_stiff = edge_stiff + product(coupled_stiff.T, end_rows)
    live_rows = (lax.iota(jnp.int32, blocks_total * block_width) < live_count * block_width).astype(
        jnp.float32
    )
    flattened = constraint.reshape(blocks_total * block_width, constraint.shape[2])
    weighted = flattened * (inner_mass * live_rows)[:, None]
    reduced_mass = jnp.diag(edge_mass) + product(flattened.T, weighted)
    coupled_modes = product((inner_modes * live_rows[:, None]).T, weighted)
    return (reduced_stiff, reduced_mass, coupled_modes)


def on_device(
    interior_stiffness,
    interior_links,
    coupling_stiffness,
    interface_stiffness,
    interior_mass,
    interface_mass,
    interior_modes,
    interior_blocks,
    interface_blocks,
    parent_modes,
):
    parent_width = PB * BLOCK
    groups = lax.axis_size("grp")
    members_count = lax.axis_size("dev")
    devices = groups * members_count
    local_count = interior_blocks.shape[0]

    def reduce_member(member):
        (
            diag_blocks,
            link_blocks,
            coupled_stiff,
            edge_stiff,
            inner_mass,
            edge_mass,
            inner_modes,
            live_count,
        ) = member
        factors, crossings = eliminate_padded(diag_blocks, link_blocks, live_count)
        constraint = solve_padded(factors, crossings, coupled_stiff, live_count)
        return project_component(
            constraint, coupled_stiff, edge_stiff, inner_mass, edge_mass, inner_modes, live_count
        )

    members = (
        interior_stiffness,
        interior_links,
        coupling_stiffness,
        interface_stiffness,
        interior_mass,
        interface_mass,
        interior_modes,
        interior_blocks,
    )
    reduced_stiff, reduced_mass, coupling = lax.map(reduce_member, members)
    per_block = devices // PB
    owned_rows = BLOCK // per_block
    matches = (interface_blocks[:, :, None] == lax.iota(jnp.int32, PB)[None, None, :]).astype(
        jnp.float32
    )

    def spread(reduced):
        pieces = reduced.reshape(local_count, NBB, per_block, owned_rows, reduced.shape[2])
        routed = jnp.einsum("cab,cajrn->bjcrn", matches, pieces, precision=lax.Precision.HIGHEST)
        return routed.reshape(devices, local_count, owned_rows, reduced.shape[2])

    column_map = jnp.broadcast_to(matches[None], (devices,) + matches.shape)
    stiff_in, mass_in, map_in = (
        lax.all_to_all(
            spread(reduced_stiff), ("grp", "dev"), split_axis=0, concat_axis=0, tiled=True
        ),
        lax.all_to_all(
            spread(reduced_mass), ("grp", "dev"), split_axis=0, concat_axis=0, tiled=True
        ),
        lax.all_to_all(column_map, ("grp", "dev"), split_axis=0, concat_axis=0, tiled=True),
    )

    def settle(received):
        pieces = received.reshape(devices, local_count, owned_rows, NBB, BLOCK)
        placed = jnp.einsum("scrak,scap->rpk", pieces, map_in, precision=lax.Precision.HIGHEST)
        return placed.reshape(owned_rows, parent_width)

    stiff_rows = settle(stiff_in)
    mass_rows = settle(mass_in)
    total_components = local_count * devices
    scaling = (PB / (total_components * NBB)) ** 0.5
    parent_stiffness = stiff_rows * scaling
    parent_mass = mass_rows * scaling
    segment = lax.all_gather(parent_modes, ("grp", "dev"), axis=0, tiled=True)
    stiff_modes = product(parent_stiffness, segment)
    mass_modes = product(parent_mass, segment)
    local_stiff = product(parent_modes.T, stiff_modes)
    local_mass = product(parent_modes.T, mass_modes)
    modal_stiffness, modal_mass = lax.psum((local_stiff, local_mass), ("grp", "dev"))
    return (parent_stiffness, parent_mass, coupling, modal_stiffness, modal_mass)


def solution(mesh):
    placed = (
        P(("grp", "dev"), None, None, None),
        P(("grp", "dev"), None, None, None),
        P(("grp", "dev"), None, None),
        P(("grp", "dev"), None, None),
        P(("grp", "dev"), None),
        P(("grp", "dev"), None),
        P(("grp", "dev"), None, None),
        P(("grp", "dev")),
        P(("grp", "dev"), None),
        P(("grp", "dev"), None),
    )
    return jax.shard_map(
        on_device,
        mesh=mesh,
        in_specs=placed,
        out_specs=(
            P(("grp", "dev"), None),
            P(("grp", "dev"), None),
            P(("grp", "dev"), None, None),
            P(),
            P(),
        ),
        check_vma=False,
    )
```

profile of v0, /device:TPU:0, one launch (start us, length us, event | category | flops | bytes accessed | tf_op | source)
XLA Modules:
  0.0 904.7 jit_solution(10418599433198816955)
XLA Ops:
  8.6 7.3 all-to-all-start
  15.9 615.4 %while.86 = (s32[]{:T(128)}, f32[2,256,256]{2,1,0:T(8,128)}, f32[2,256,256]{2,1,0:T(8,128)}, f32[2,256,256]{2,1,0:T(8,128)}, f32[2,256,256]{2,1,0:T(8,128)}, /*i...) while((s32[]{:T(128)}, f32[2,256,256]{2,1,0:T(8,128)}, ...), condition=%wide.region_7.8_spmd, body=%wide.region_0.7_spmd.sunk | while | flops 1915033728 | bytes 43467348 | solution.py:129
  20.4 189.0 %while.87 = (s32[]{:T(128)}, f32[128,128]{1,0:T(8,128)S(1)}, f32[8,128,128]{2,1,0:T(8,128)S(1)}, f32[8,128,128]{2,1,0:T(8,128)S(1)}, f32[8,128,128]{1,2,0:T(8,128)S(1)}, /*index=5*/f32[8,128,128]{2,1,0:T(8,128)S(1)}, s32[]{:T(128)}) while((s32[]{:T(128)}, f32[128,128]{1,0:T(8,128)S(1)}, f32[8,128,128]{2,1,0:T(8,128)S(1)}, ...), condition=%wide.region_4.4_spmd, body=%wide.region_1.3_spmd.sunk | while | flops 50512000 | bytes 1247319 | solution.py:37
  20.4 9.8 %custom-call.36 = f32[1,128,128]{1,2,0:T(8,128)S(1)} custom-call(f32[1,128,128]{2,1,0:T(8,128)S(1)} %select_bitcast_fusion.2), custom_call_target="InvertDiagBlocksLowerTriangular" | custom-call | tf_op jit(solution)/shard_map/while/body/eval_jaxpr/while/body/eval_jaxpr/triangular_solve | solution.py:30
  30.8 11.7 %cholesky.54 = f32[128,128]{1,0:T(8,128)S(1)} custom-call(f32[128,128]{1,0:T(8,128)S(1)} %fusion.112), custom_call_target="Cholesky" | custom-call | tf_op jit(solution)/shard_map/while/body/eval_jaxpr/while/body/eval_jaxpr/jit(cholesky)/cholesky | solution.py:34
  44.0 9.8 %custom-call.36 = f32[1,128,128]{1,2,0:T(8,128)S(1)} custom-call(f32[1,128,128]{2,1,0:T(8,128)S(1)} %select_bitcast_fusion.2), custom_call_target="InvertDiagBlocksLowerTriangular" | custom-call | tf_op jit(solution)/shard_map/while/body/eval_jaxpr/while/body/eval_jaxpr/triangular_solve | solution.py:30
  54.5 11.7 %cholesky.54 = f32[128,128]{1,0:T(8,128)S(1)} custom-call(f32[128,128]{1,0:T(8,128)S(1)} %fusion.112), custom_call_target="Cholesky" | custom-call | tf_op jit(solution)/shard_map/while/body/eval_jaxpr/while/body/eval_jaxpr/jit(cholesky)/cholesky | solution.py:34
  67.7 9.8 %custom-call.36 = f32[1,128,128]{1,2,0:T(8,128)S(1)} custom-call(f32[1,128,128]{2,1,0:T(8,128)S(1)} %select_bitcast_fusion.2), custom_call_target="InvertDiagBlocksLowerTriangular" | custom-call | tf_op jit(solution)/shard_map/while/body/eval_jaxpr/while/body/eval_jaxpr/triangular_solve | solution.py:30
  78.1 11.7 %cholesky.54 = f32[128,128]{1,0:T(8,128)S(1)} custom-call(f32[128,128]{1,0:T(8,128)S(1)} %fusion.112), custom_call_target="Cholesky" | custom-call | tf_op jit(solution)/shard_map/while/body/eval_jaxpr/while/body/eval_jaxpr/jit(cholesky)/cholesky | solution.py:34
  91.3 9.8 %custom-call.36 = f32[1,128,128]{1,2,0:T(8,128)S(1)} custom-call(f32[1,128,128]{2,1,0:T(8,128)S(1)} %select_bitcast_fusion.2), custom_call_target="InvertDiagBlocksLowerTriangular" | custom-call | tf_op jit(solution)/shard_map/while/body/eval_jaxpr/while/body/eval_jaxpr/triangular_solve | solution.py:30
  101.7 11.7 %cholesky.54 = f32[128,128]{1,0:T(8,128)S(1)} custom-call(f32[128,128]{1,0:T(8,128)S(1)} %fusion.112), custom_call_target="Cholesky" | custom-call | tf_op jit(solution)/shard_map/while/body/eval_jaxpr/while/body/eval_jaxpr/jit(cholesky)/cholesky | solution.py:34
  114.9 9.8 %custom-call.36 = f32[1,128,128]{1,2,0:T(8,128)S(1)} custom-call(f32[1,128,128]{2,1,0:T(8,128)S(1)} %select_bitcast_fusion.2), custom_call_target="InvertDiagBlocksLowerTriangular" | custom-call | tf_op jit(solution)/shard_map/while/body/eval_jaxpr/while/body/eval_jaxpr/triangular_solve | solution.py:30
  125.3 11.7 %cholesky.54 = f32[128,128]{1,0:T(8,128)S(1)} custom-call(f32[128,128]{1,0:T(8,128)S(1)} %fusion.112), custom_call_target="Cholesky" | custom-call | tf_op jit(solution)/shard_map/while/body/eval_jaxpr/while/body/eval_jaxpr/jit(cholesky)/cholesky | solution.py:34
  138.5 9.8 %custom-call.36 = f32[1,128,128]{1,2,0:T(8,128)S(1)} custom-call(f32[1,128,128]{2,1,0:T(8,128)S(1)} %select_bitcast_fusion.2), custom_call_target="InvertDiagBlocksLowerTriangular" | custom-call | tf_op jit(solution)/shard_map/while/body/eval_jaxpr/while/body/eval_jaxpr/triangular_solve | solution.py:30
  149.0 11.7 %cholesky.54 = f32[128,128]{1,0:T(8,128)S(1)} custom-call(f32[128,128]{1,0:T(8,128)S(1)} %fusion.112), custom_call_target="Cholesky" | custom-call | tf_op jit(solution)/shard_map/while/body/eval_jaxpr/while/body/eval_jaxpr/jit(cholesky)/cholesky | solution.py:34
  162.2 9.8 %custom-call.36 = f32[1,128,128]{1,2,0:T(8,128)S(1)} custom-call(f32[1,128,128]{2,1,0:T(8,128)S(1)} %select_bitcast_fusion.2), custom_call_target="InvertDiagBlocksLowerTriangular" | custom-call | tf_op jit(solution)/shard_map/while/body/eval_jaxpr/while/body/eval_jaxpr/triangular_solve | solution.py:30
  172.6 11.7 %cholesky.54 = f32[128,128]{1,0:T(8,128)S(1)} custom-call(f32[128,128]{1,0:T(8,128)S(1)} %fusion.112), custom_call_target="Cholesky" | custom-call | tf_op jit(solution)/shard_map/while/body/eval_jaxpr/while/body/eval_jaxpr/jit(cholesky)/cholesky | solution.py:34
  185.8 9.8 %custom-call.36 = f32[1,128,128]{1,2,0:T(8,128)S(1)} custom-call(f32[1,128,128]{2,1,0:T(8,128)S(1)} %select_bitcast_fusion.2), custom_call_target="InvertDiagBlocksLowerTriangular" | custom-call | tf_op jit(solution)/shard_map/while/body/eval_jaxpr/while/body/eval_jaxpr/triangular_solve | solution.py:30
  196.2 11.7 %cholesky.54 = f32[128,128]{1,0:T(8,128)S(1)} custom-call(f32[128,128]{1,0:T(8,128)S(1)} %fusion.112), custom_call_target="Cholesky" | custom-call | tf_op jit(solution)/shard_map/while/body/eval_jaxpr/while/body/eval_jaxpr/jit(cholesky)/cholesky | solution.py:34
  210.7 9.8 %custom-call.35 = f32[1,128,128]{1,2,0:T(8,128)S(1)} custom-call(f32[1,128,128]{2,1,0:T(8,128)S(1)} %dynamic-slice_select_fusion.4), custom_call_target="InvertDiagBlocksLowerTriangular" | custom-call | tf_op jit(solution)/shard_map/while/body/eval_jaxpr/triangular_solve | solution.py:46
  221.1 94.5 %while.88 = (s32[]{:T(128)}, f32[128,256]{1,0:T(8,128)S(1)}, f32[8,128,256]{2,1,0:T(8,128)S(1)}, f32[8,128,128]{2,1,0:T(8,128)S(1)}, s32[8]{0:T(128)S(1)}, /*ind...) while((s32[]{:T(128)}, f32[128,256]{1,0:T(8,128)S(1)}, ...), condition=%wide.region_6.6_spmd, body=%wide.region_5.5_spmd.sunk | while | flops 100761600 | bytes 1048723 | solution.py:61
  222.8 9.8 %custom-call.37 = f32[1,128,128]{1,2,0:T(8,128)S(1)} custom-call(f32[1,128,128]{2,1,0:T(8,128)S(1)} %dynamic-slice_select_fusion.5), custom_call_target="InvertDiagBlocksLowerTriangular" | custom-call | tf_op jit(solution)/shard_map/while/body/eval_jaxpr/while/body/eval_jaxpr/triangular_solve | solution.py:56
  234.6 9.8 %custom-call.37 = f32[1,128,128]{1,2,0:T(8,128)S(1)} custom-call(f32[1,128,128]{2,1,0:T(8,128)S(1)} %dynamic-slice_select_fusion.5), custom_call_target="InvertDiagBlocksLowerTriangular" | custom-call | tf_op jit(solution)/shard_map/while/body/eval_jaxpr/while/body/eval_jaxpr/triangular_solve | solution.py:56
  246.4 9.8 %custom-call.37 = f32[1,128,128]{1,2,0:T(8,128)S(1)} custom-call(f32[1,128,128]{2,1,0:T(8,128)S(1)} %dynamic-slice_select_fusion.5), custom_call_target="InvertDiagBlocksLowerTriangular" | custom-call | tf_op jit(solution)/shard_map/while/body/eval_jaxpr/while/body/eval_jaxpr/triangular_solve | solution.py:56
  258.2 9.8 %custom-call.37 = f32[1,128,128]{1,2,0:T(8,128)S(1)} custom-call(f32[1,128,128]{2,1,0:T(8,128)S(1)} %dynamic-slice_select_fusion.5), custom_call_target="InvertDiagBlocksLowerTriangular" | custom-call | tf_op jit(solution)/shard_map/while/body/eval_jaxpr/while/body/eval_jaxpr/triangular_solve | solution.py:56
  270.0 9.8 %custom-call.37 = f32[1,128,128]{1,2,0:T(8,128)S(1)} custom-call(f32[1,128,128]{2,1,0:T(8,128)S(1)} %dynamic-slice_select_fusion.5), custom_call_target="InvertDiagBlocksLowerTriangular" | custom-call | tf_op jit(solution)/shard_map/while/body/eval_jaxpr/while/body/eval_jaxpr/triangular_solve | solution.py:56
  281.9 9.8 %custom-call.37 = f32[1,128,128]{1,2,0:T(8,128)S(1)} custom-call(f32[1,128,128]{2,1,0:T(8,128)S(1)} %dynamic-slice_select_fusion.5), custom_call_target="InvertDiagBlocksLowerTriangular" | custom-call | tf_op jit(solution)/shard_map/while/body/eval_jaxpr/while/body/eval_jaxpr/triangular_solve | solution.py:56
  293.7 9.8 %custom-call.37 = f32[1,128,128]{1,2,0:T(8,128)S(1)} custom-call(f32[1,128,128]{2,1,0:T(8,128)S(1)} %dynamic-slice_select_fusion.5), custom_call_target="InvertDiagBlocksLowerTriangular" | custom-call | tf_op jit(solution)/shard_map/while/body/eval_jaxpr/while/body/eval_jaxpr/triangular_solve | solution.py:56
  305.5 9.8 %custom-call.37 = f32[1,128,128]{1,2,0:T(8,128)S(1)} custom-call(f32[1,128,128]{2,1,0:T(8,128)S(1)} %dynamic-slice_select_fusion.5), custom_call_target="InvertDiagBlocksLowerTriangular" | custom-call | tf_op jit(solution)/shard_map/while/body/eval_jaxpr/while/body/eval_jaxpr/triangular_solve | solution.py:56
  320.9 2.7 fusion.107
  328.0 189.0 %while.87 = (s32[]{:T(128)}, f32[128,128]{1,0:T(8,128)S(1)}, f32[8,128,128]{2,1,0:T(8,128)S(1)}, f32[8,128,128]{2,1,0:T(8,128)S(1)}, f32[8,128,128]{1,2,0:T(8,128)S(1)}, /*index=5*/f32[8,128,128]{2,1,0:T(8,128)S(1)}, s32[]{:T(128)}) while((s32[]{:T(128)}, f32[128,128]{1,0:T(8,128)S(1)}, f32[8,128,128]{2,1,0:T(8,128)S(1)}, ...), condition=%wide.region_4.4_spmd, body=%wide.region_1.3_spmd.sunk | while | flops 50512000 | bytes 1247319 | solution.py:37
  328.1 9.8 %custom-call.36 = f32[1,128,128]{1,2,0:T(8,128)S(1)} custom-call(f32[1,128,128]{2,1,0:T(8,128)S(1)} %select_bitcast_fusion.2), custom_call_target="InvertDiagBlocksLowerTriangular" | custom-call | tf_op jit(solution)/shard_map/while/body/eval_jaxpr/while/body/eval_jaxpr/triangular_solve | solution.py:30
  338.5 11.7 %cholesky.54 = f32[128,128]{1,0:T(8,128)S(1)} custom-call(f32[128,128]{1,0:T(8,128)S(1)} %fusion.112), custom_call_target="Cholesky" | custom-call | tf_op jit(solution)/shard_map/while/body/eval_jaxpr/while/body/eval_jaxpr/jit(cholesky)/cholesky | solution.py:34
  351.7 9.8 %custom-call.36 = f32[1,128,128]{1,2,0:T(8,128)S(1)} custom-call(f32[1,128,128]{2,1,0:T(8,128)S(1)} %select_bitcast_fusion.2), custom_call_target="InvertDiagBlocksLowerTriangular" | custom-call | tf_op jit(solution)/shard_map/while/body/eval_jaxpr/while/body/eval_jaxpr/triangular_solve | solution.py:30
  362.1 11.7 %cholesky.54 = f32[128,128]{1,0:T(8,128)S(1)} custom-call(f32[128,128]{1,0:T(8,128)S(1)} %fusion.112), custom_call_target="Cholesky" | custom-call | tf_op jit(solution)/shard_map/while/body/eval_jaxpr/while/body/eval_jaxpr/jit(cholesky)/cholesky | solution.py:34
  375.3 9.8 %custom-call.36 = f32[1,128,128]{1,2,0:T(8,128)S(1)} custom-call(f32[1,128,128]{2,1,0:T(8,128)S(1)} %select_bitcast_fusion.2), custom_call_target="InvertDiagBlocksLowerTriangular" | custom-call | tf_op jit(solution)/shard_map/while/body/eval_jaxpr/while/body/eval_jaxpr/triangular_solve | solution.py:30
  385.7 11.7 %cholesky.54 = f32[128,128]{1,0:T(8,128)S(1)} custom-call(f32[128,128]{1,0:T(8,128)S(1)} %fusion.112), custom_call_target="Cholesky" | custom-call | tf_op jit(solution)/shard_map/while/body/eval_jaxpr/while/body/eval_jaxpr/jit(cholesky)/cholesky | solution.py:34
  399.0 9.8 %custom-call.36 = f32[1,128,128]{1,2,0:T(8,128)S(1)} custom-call(f32[1,128,128]{2,1,0:T(8,128)S(1)} %select_bitcast_fusion.2), custom_call_target="InvertDiagBlocksLowerTriangular" | custom-call | tf_op jit(solution)/shard_map/while/body/eval_jaxpr/while/body/eval_jaxpr/triangular_solve | solution.py:30
  409.4 11.7 %cholesky.54 = f32[128,128]{1,0:T(8,128)S(1)} custom-call(f32[128,128]{1,0:T(8,128)S(1)} %fusion.112), custom_call_target="Cholesky" | custom-call | tf_op jit(solution)/shard_map/while/body/eval_jaxpr/while/body/eval_jaxpr/jit(cholesky)/cholesky | solution.py:34
  422.6 9.8 %custom-call.36 = f32[1,128,128]{1,2,0:T(8,128)S(1)} custom-call(f32[1,128,128]{2,1,0:T(8,128)S(1)} %select_bitcast_fusion.2), custom_call_target="InvertDiagBlocksLowerTriangular" | custom-call | tf_op jit(solution)/shard_map/while/body/eval_jaxpr/while/body/eval_jaxpr/triangular_solve | solution.py:30
  433.0 11.7 %cholesky.54 = f32[128,128]{1,0:T(8,128)S(1)} custom-call(f32[128,128]{1,0:T(8,128)S(1)} %fusion.112), custom_call_target="Cholesky" | custom-call | tf_op jit(solution)/shard_map/while/body/eval_jaxpr/while/body/eval_jaxpr/jit(cholesky)/cholesky | solution.py:34
  446.2 9.8 %custom-call.36 = f32[1,128,128]{1,2,0:T(8,128)S(1)} custom-call(f32[1,128,128]{2,1,0:T(8,128)S(1)} %select_bitcast_fusion.2), custom_call_target="InvertDiagBlocksLowerTriangular" | custom-call | tf_op jit(solution)/shard_map/while/body/eval_jaxpr/while/body/eval_jaxpr/triangular_solve | solution.py:30
  456.6 11.7 %cholesky.54 = f32[128,128]{1,0:T(8,128)S(1)} custom-call(f32[128,128]{1,0:T(8,128)S(1)} %fusion.112), custom_call_target="Cholesky" | custom-call | tf_op jit(solution)/shard_map/while/body/eval_jaxpr/while/body/eval_jaxpr/jit(cholesky)/cholesky | solution.py:34
  469.8 9.8 %custom-call.36 = f32[1,128,128]{1,2,0:T(8,128)S(1)} custom-call(f32[1,128,128]{2,1,0:T(8,128)S(1)} %select_bitcast_fusion.2), custom_call_target="InvertDiagBlocksLowerTriangular" | custom-call | tf_op jit(solution)/shard_map/while/body/eval_jaxpr/while/body/eval_jaxpr/triangular_solve | solution.py:30
  480.3 11.7 %cholesky.54 = f32[128,128]{1,0:T(8,128)S(1)} custom-call(f32[128,128]{1,0:T(8,128)S(1)} %fusion.112), custom_call_target="Cholesky" | custom-call | tf_op jit(solution)/shard_map/while/body/eval_jaxpr/while/body/eval_jaxpr/jit(cholesky)/cholesky | solution.py:34
  493.5 9.8 %custom-call.36 = f32[1,128,128]{1,2,0:T(8,128)S(1)} custom-call(f32[1,128,128]{2,1,0:T(8,128)S(1)} %select_bitcast_fusion.2), custom_call_target="InvertDiagBlocksLowerTriangular" | custom-call | tf_op jit(solution)/shard_map/while/body/eval_jaxpr/while/body/eval_jaxpr/triangular_solve | solution.py:30
  503.9 11.7 %cholesky.54 = f32[128,128]{1,0:T(8,128)S(1)} custom-call(f32[128,128]{1,0:T(8,128)S(1)} %fusion.112), custom_call_target="Cholesky" | custom-call | tf_op jit(solution)/shard_map/while/body/eval_jaxpr/while/body/eval_jaxpr/jit(cholesky)/cholesky | solution.py:34
  518.4 9.8 %custom-call.35 = f32[1,128,128]{1,2,0:T(8,128)S(1)} custom-call(f32[1,128,128]{2,1,0:T(8,128)S(1)} %dynamic-slice_select_fusion.4), custom_call_target="InvertDiagBlocksLowerTriangular" | custom-call | tf_op jit(solution)/shard_map/while/body/eval_jaxpr/triangular_solve | solution.py:46
  528.7 94.5 %while.88 = (s32[]{:T(128)}, f32[128,256]{1,0:T(8,128)S(1)}, f32[8,128,256]{2,1,0:T(8,128)S(1)}, f32[8,128,128]{2,1,0:T(8,128)S(1)}, s32[8]{0:T(128)S(1)}, /*ind...) while((s32[]{:T(128)}, f32[128,256]{1,0:T(8,128)S(1)}, ...), condition=%wide.region_6.6_spmd, body=%wide.region_5.5_spmd.sunk | while | flops 100761600 | bytes 1048723 | solution.py:61
  530.5 9.8 %custom-call.37 = f32[1,128,128]{1,2,0:T(8,128)S(1)} custom-call(f32[1,128,128]{2,1,0:T(8,128)S(1)} %dynamic-slice_select_fusion.5), custom_call_target="InvertDiagBlocksLowerTriangular" | custom-call | tf_op jit(solution)/shard_map/while/body/eval_jaxpr/while/body/eval_jaxpr/triangular_solve | solution.py:56
  542.3 9.8 %custom-call.37 = f32[1,128,128]{1,2,0:T(8,128)S(1)} custom-call(f32[1,128,128]{2,1,0:T(8,128)S(1)} %dynamic-slice_select_fusion.5), custom_call_target="InvertDiagBlocksLowerTriangular" | custom-call | tf_op jit(solution)/shard_map/while/body/eval_jaxpr/while/body/eval_jaxpr/triangular_solve | solution.py:56
  554.1 9.8 %custom-call.37 = f32[1,128,128]{1,2,0:T(8,128)S(1)} custom-call(f32[1,128,128]{2,1,0:T(8,128)S(1)} %dynamic-slice_select_fusion.5), custom_call_target="InvertDiagBlocksLowerTriangular" | custom-call | tf_op jit(solution)/shard_map/while/body/eval_jaxpr/while/body/eval_jaxpr/triangular_solve | solution.py:56
  565.9 9.8 %custom-call.37 = f32[1,128,128]{1,2,0:T(8,128)S(1)} custom-call(f32[1,128,128]{2,1,0:T(8,128)S(1)} %dynamic-slice_select_fusion.5), custom_call_target="InvertDiagBlocksLowerTriangular" | custom-call | tf_op jit(solution)/shard_map/while/body/eval_jaxpr/while/body/eval_jaxpr/triangular_solve | solution.py:56
  577.7 9.8 %custom-call.37 = f32[1,128,128]{1,2,0:T(8,128)S(1)} custom-call(f32[1,128,128]{2,1,0:T(8,128)S(1)} %dynamic-slice_select_fusion.5), custom_call_target="InvertDiagBlocksLowerTriangular" | custom-call | tf_op jit(solution)/shard_map/while/body/eval_jaxpr/while/body/eval_jaxpr/triangular_solve | solution.py:56
  589.5 9.8 %custom-call.37 = f32[1,128,128]{1,2,0:T(8,128)S(1)} custom-call(f32[1,128,128]{2,1,0:T(8,128)S(1)} %dynamic-slice_select_fusion.5), custom_call_target="InvertDiagBlocksLowerTriangular" | custom-call | tf_op jit(solution)/shard_map/while/body/eval_jaxpr/while/body/eval_jaxpr/triangular_solve | solution.py:56
  601.3 9.8 %custom-call.37 = f32[1,128,128]{1,2,0:T(8,128)S(1)} custom-call(f32[1,128,128]{2,1,0:T(8,128)S(1)} %dynamic-slice_select_fusion.5), custom_call_target="InvertDiagBlocksLowerTriangular" | custom-call | tf_op jit(solution)/shard_map/while/body/eval_jaxpr/while/body/eval_jaxpr/triangular_solve | solution.py:56
  613.1 9.8 %custom-call.37 = f32[1,128,128]{1,2,0:T(8,128)S(1)} custom-call(f32[1,128,128]{2,1,0:T(8,128)S(1)} %dynamic-slice_select_fusion.5), custom_call_target="InvertDiagBlocksLowerTriangular" | custom-call | tf_op jit(solution)/shard_map/while/body/eval_jaxpr/while/body/eval_jaxpr/triangular_solve | solution.py:56
  635.7 5.8 all-to-all-start.1
  645.9 45.6 %all-to-all-done.1 = f32[32,2,32,256]{3,2,1,0:T(8,128)S(1)} async-done(((f32[32,2,32,256]{3,2,1,0:T(8,128)}), f32[32,2,32,256]{3,2,1,0:T(8,128)S(1)}, u32[]{:S(2)}, u32[]{:S(2)}) %all-to-all-start.1) | async-done | bytes 2097184 | tf_op jit(solution)/shard_map/all_to_all | solution.py:143
  691.5 3.5 all-to-all-start.2
  697.9 49.1 %all-to-all-done.2 = f32[32,2,32,256]{3,2,1,0:T(8,128)} async-done(((f32[32,2,32,256]{3,2,1,0:T(8,128)}), f32[32,2,32,256]{3,2,1,0:T(8,128)}, u32[]{:S(2)}, u32[]{:S(2)}) %all-to-all-start.2) | async-done | bytes 2097184 | tf_op jit(solution)/shard_map/all_to_all | solution.py:146
  747.0 3.2 reshape.156
  755.3 4.5 all-gather.2.cloned.1.call-done
  764.6 129.6 %all-reduce.5.cloned.1.call-done = (f32[256,256]{0,1:T(8,128)}, f32[256,256]{0,1:T(8,128)}) async-done(((f32[256,256]{0,1:T(8,128)}, f32[256,256]{0,1:T(8,128)}), (f32[256,256]{0,1:T(8,128)}, f32[256,256]{0,1:T(8,128)})) %all-reduce.5.cloned.1.call-update) | async-done | bytes 524304 | tf_op jit(solution)/shard_map/psum | solution.py:168
  (327 shorter events, 100.6 us)
Async XLA Ops:
  8.6 627.1 %all-to-all-start = ((f32[32,2,2,8]{3,1,2,0:T(2,128)}), f32[32,2,2,8]{3,1,2,0:T(2,128)S(1)}, u32[]{:S(2)}, u32[]{:S(2)}) async-start(f32[32,2,2,8]{3,1,2,0:T(2,128)} %broadcast_in_dim.143), calls=%async_computation | async-start | bytes 131072 | tf_op jit(solution)/shard_map/all_to_all | solution.py:149
  15.9 615.4 %copy-start.14 = (s32[2,2]{1,0:T(2,128)S(1)}, s32[2,2]{1,0:T(2,128)}, u32[]{:S(2)}) copy-start(s32[2,2]{1,0:T(2,128)} %param.24) | copy-start | bytes 52
  16.0 4.2 copy-start.4
  20.4 200.2 %copy-start.3 = (f32[2,128,256]{2,1,0:T(8,128)S(1)}, f32[2,128,256]{2,1,0:T(8,128)}, u32[]{:S(2)}) copy-start(f32[2,128,256]{2,1,0:T(8,128)} %get-tuple-element.904) | copy-start | bytes 786436 | tf_op jit(solution)/shard_map/while
  221.1 95.3 %copy-start.12 = (f32[2,1024]{1,0:T(2,128)S(1)}, f32[2,1024]{1,0:T(2,128)}, u32[]{:S(2)}) copy-start(f32[2,1024]{1,0:T(2,128)} %get-tuple-element.909) | copy-start | bytes 24580 | tf_op jit(solution)/shard_map/while
  315.6 1.6 copy-start
  316.4 1.2 copy-start.15
  316.4 3.2 copy-start.6
  316.5 3.2 copy-start.7
  316.7 4.2 copy-start.13
  319.6 1.3 copy-start.16
  320.1 0.8 copy-start.8
  323.6 4.2 copy-start.4
  328.0 200.2 %copy-start.3 = (f32[2,128,256]{2,1,0:T(8,128)S(1)}, f32[2,128,256]{2,1,0:T(8,128)}, u32[]{:S(2)}) copy-start(f32[2,128,256]{2,1,0:T(8,128)} %get-tuple-element.904) | copy-start | bytes 786436 | tf_op jit(solution)/shard_map/while
  528.7 95.3 %copy-start.12 = (f32[2,1024]{1,0:T(2,128)S(1)}, f32[2,1024]{1,0:T(2,128)}, u32[]{:S(2)}) copy-start(f32[2,1024]{1,0:T(2,128)} %get-tuple-element.909) | copy-start | bytes 24580 | tf_op jit(solution)/shard_map/while
  623.2 1.6 copy-start
  624.0 1.2 copy-start.15
  624.1 3.2 copy-start.6
  624.1 3.2 copy-start.7
  624.4 4.2 copy-start.13
  627.3 1.3 copy-start.16
  627.7 0.8 copy-start.8
  635.7 55.8 %all-to-all-start.1 = ((f32[32,2,32,256]{3,2,1,0:T(8,128)}), f32[32,2,32,256]{3,2,1,0:T(8,128)S(1)}, u32[]{:S(2)}, u32[]{:S(2)}) async-start(f32[32,2,32,256]{3,2,1,0:T(8,128)} %bitcast.205), calls=%async_computation.1 | async-start | bytes 4194304 | tf_op jit(solution)/shard_map/all_to_all | solution.py:143
  691.5 55.5 %all-to-all-start.2 = ((f32[32,2,32,256]{3,2,1,0:T(8,128)}), f32[32,2,32,256]{3,2,1,0:T(8,128)}, u32[]{:S(2)}, u32[]{:S(2)}) async-start(f32[32,2,32,256]{3,2,1,0:T(8,128)} %bitcast.204), calls=%async_computation.2 | async-start | bytes 4194304 | tf_op jit(solution)/shard_map/all_to_all | solution.py:146
  695.0 64.8 %all-gather.2.cloned.1.call-start = ((), (), s32[]{:S(2)}) async-start(), calls=%async_computation.3 | async-start | bytes 1081344 | tf_op jit(solution)/shard_map/all_gather | solution.py:163
  695.7 198.5 %all-reduce.5.cloned.1.call-start = ((), (), s32[]{:S(2)}) async-start(), calls=%async_computation.4 | async-start | bytes 1048576 | tf_op jit(solution)/shard_map/psum | solution.py:168
  697.9 52.3 %copy-start.1 = (f32[32,2,32,2,128]{4,3,2,1,0:T(2,128)S(1)}, f32[32,2,32,2,128]{4,3,2,1,0:T(2,128)}, u32[]{:S(2)}) copy-start(f32[32,2,32,2,128]{4,3,2,1,0:T(2,128)} %reshape.153) | copy-start | bytes 6291460
  750.3 2.5 copy-start.2
  752.8 9.0 copy-start.11
  755.3 142.5 %copy-start.9 = (f32[32,1024]{1,0:T(8,128)}, f32[32,1024]{1,0:T(8,128)S(1)}, u32[]{:S(2)}) copy-start(f32[32,1024]{1,0:T(8,128)S(1)} %get-tuple-element.594) | copy-start | bytes 393220
  755.3 142.5 %copy-start.10 = (f32[32,1024]{1,0:T(8,128)}, f32[32,1024]{1,0:T(8,128)S(1)}, u32[]{:S(2)}) copy-start(f32[32,1024]{1,0:T(8,128)S(1)} %get-tuple-element.595) | copy-start | bytes 393220
  759.8 3.0 copy-start.5
Sparse Core Ops, SparseCore 0:
  698.8 60.9 all-gather.1
  765.9 128.3 all-reduce.4
where the time goes:
time: 906 us; the launch traced here: 905 us
  other arithmetic  549 us (61%)
  waiting for transfers between devices  229 us (25%)
  matrix products  42.4 us (5%)
  local copies, waits for them, and re-layouts  35 us (4%)
  loops' own time  17.7 us (2%)
  starting transfers between devices  16.7 us (2%)
  between operations  14.2 us (2%)
    another operation x48, other arithmetic, eliminate_advance(): factor = jnp.linalg.cholesky(schur_part)  199 us
    another operation x32, other arithmetic, solve_advance(): lax.linalg.triangular_solve(factor, right_side, left_side=True, lower=Tru...  157 us
    another operation x32, other arithmetic, eliminate_advance(): lax.linalg.triangular_solve(previous, block_low, left_side=False, lower=T...  157 us
    psum x1, waiting for transfers between devices, on_device(): lax.psum((local_stiff, local_mass), ('grp', 'dev'))  130 us
    all_to_all x1, waiting for transfers between devices, on_device(): lax.all_to_all(spread(reduced_mass), ('grp', 'dev'), split_axis=0, concat...  49.1 us
    all_to_all x1, waiting for transfers between devices, on_device(): lax.all_to_all(spread(reduced_stiff), ('grp', 'dev'), split_axis=0, conca...  45.6 us
    dot_general x42, matrix products, product(): jnp.dot(left, right, precision=lax.Precision.HIGHEST, preferred_element_t...  24.4 us
    another operation x4, other arithmetic, solve_padded(): lax.linalg.triangular_solve(end_factor, coupled_stiff, left_side=True, lo...  19.6 us
  transfers between devices with their start and end apart: 5, of which 4 were waited for; matrix products, arithmetic and copies ran while one was open for 68% of the time, Pallas kernels for 0%

commit v1 on v0

v1 whole, which is shorter than its diff:
```python
import functools
import jax
import jax.numpy as jnp
from jax import lax
from jax.experimental import pallas as pl
from jax.experimental.pallas import tpu as pltpu
from jax.sharding import PartitionSpec as P

AXES = ("grp", "dev")
PB = 8

PANEL = 16


def mm(left, right):
    return lax.dot_general(
        left, right, (((1,), (0,)), ((), ())),
        precision=lax.Precision.HIGHEST, preferred_element_type=jnp.float32,
    )


def sweep_panel(work, chains, width, index):
    start = index * PANEL
    rows = pl.ds(start, PANEL)
    lane = lax.broadcasted_iota(jnp.int32, (PANEL, width), 1)
    sub = lax.broadcasted_iota(jnp.int32, (PANEL, width), 0)
    chain_of = (lane // PANEL) % chains
    panels = [work[g, rows, :] for g in range(chains)]
    columns = []
    for j in range(PANEL):
        packed = None
        for g in range(chains):
            column = jnp.broadcast_to(panels[g][:, start + j : start + j + 1], (PANEL, width))
            packed = column if packed is None else jnp.where(chain_of == g, column, packed)
        columns.append(packed)
    for s in range(PANEL):
        here = columns[s]
        pivot = here[s : s + 1, :]
        inverse = 1.0 / pivot
        scaled = here * inverse
        lowered = jnp.where(sub == s, here - 1.0, here)
        for j in range(PANEL):
            if j != s:
                columns[j] = columns[j] - lowered * scaled[j : j + 1, :]
        columns[s] = jnp.where(sub == s, -inverse, scaled)
    compact = jnp.zeros((PANEL, width), jnp.float32)
    for j in range(PANEL):
        compact = jnp.where(lane % PANEL == j, columns[j], compact)
    stacked = jnp.concatenate(
        [jnp.where(lane // PANEL == g, compact, 0.0) for g in range(chains)], 0
    )
    mine = lane // PANEL == index
    unit = jnp.where(lane - start == sub, -1.0, 0.0)
    sources = [jnp.where(mine, unit, panels[g]) for g in range(chains)]
    fill = width - chains * PANEL
    if fill > 0:
        sources.append(jnp.zeros((fill, width), jnp.float32))
    reduced = mm(stacked, jnp.concatenate(sources, 0))
    mine_all = lax.broadcasted_iota(jnp.int32, (width, width), 1) // PANEL == index
    for g in range(chains):
        part = reduced[g * PANEL : (g + 1) * PANEL]
        pieces = []
        if start > 0:
            pieces.append(jnp.zeros((start, width), jnp.float32))
        pieces.append(part)
        if start + PANEL < width:
            pieces.append(jnp.zeros((width - start - PANEL, width), jnp.float32))
        weights = jnp.concatenate(pieces, 0)
        current = work[g]
        work[g] = jnp.where(mine_all, 0.0, current) + mm(current, weights)
        work[g, rows, :] = -part


def reduce_kernel(
    counts, place, diag, links, coupled, edge, inner_mass, edge_mass, modes,
    reduced_out, coupling_out, *rest,
):
    pieces_out = rest[:-6]
    work, state, moved, ahead, source, solved = rest[-6:]
    members, blocks, width, _ = diag.shape
    chains = 2 * members
    columns_total = coupled.shape[2]
    live = [counts[c] for c in range(members)]
    middle = [live[c] // 2 for c in range(members)]
    below = [live[c] - 1 - middle[c] for c in range(members)]
    levels = middle[0]
    for c in range(1, members):
        levels = jnp.maximum(levels, middle[c])
    for c in range(members):
        work[2 * c] = diag[c, 0]
        state[2 * c] = diag[c, 0]
        work[2 * c + 1] = diag[c, live[c] - 1]
        state[2 * c + 1] = diag[c, live[c] - 1]
        source[c] = coupled[c]
        solved[c] = jnp.zeros(solved.shape[1:], jnp.float32)

    def level(t, carry):
        for index in range(width // PANEL):
            sweep_panel(work, chains, width, index)

        @pl.when(t < levels)
        def _():
            for c in range(members):
                top = jnp.minimum(t, blocks - 2)
                top_after = jnp.minimum(t + 1, blocks - 1)
                bottom = jnp.maximum(live[c] - 2 - t, 0)
                link_top = links[c, top]
                link_bottom = links[c, bottom]
                moved_top = mm(work[2 * c], link_top.T)
                moved_bottom = mm(work[2 * c + 1], link_bottom)
                moved[t, 2 * c] = moved_top
                moved[t, 2 * c + 1] = moved_bottom
                moved_t = moved_bottom.T
                ahead[t, c] = mm(work[2 * c + 1], source[c])
                next_top = diag[c, top_after] + mm(link_top, moved_top)
                next_bottom = diag[c, bottom] + mm(moved_t, link_bottom)
                next_source = mm(moved_t, source[c])
                next_top = jnp.where(t < middle[c], next_top, state[2 * c])
                next_bottom = jnp.where(t < below[c], next_bottom, state[2 * c + 1])
                source[c] = jnp.where(t < below[c], next_source, source[c])
                state[2 * c] = next_top
                state[2 * c + 1] = next_bottom
                joined = next_top - (diag[c, middle[c]] - next_bottom)
                last = t == levels - 1
                work[2 * c] = jnp.where(last, joined, next_top)
                work[2 * c + 1] = jnp.where(last, joined, next_bottom)

        return carry

    lax.fori_loop(0, levels + 1, level, 0)
    for c in range(members):
        solved[c, middle[c]] = mm(work[2 * c], source[c])

    def back(s, carry):
        for c in range(members):
            top = middle[c] - 1 - s
            top_live = top >= 0
            top_safe = jnp.maximum(top, 0)
            upper = mm(moved[top_safe, 2 * c], solved[c, top_safe + 1])
            bottom = middle[c] + 1 + s
            bottom_live = bottom < live[c]
            bottom_safe = jnp.where(bottom_live, bottom, 1)
            step = jnp.where(bottom_live, live[c] - 1 - bottom, 0)
            lower = ahead[step, c] + mm(moved[step, 2 * c + 1], solved[c, bottom_safe - 1])
            solved[c, jnp.where(top_live, top, blocks)] = upper
            solved[c, jnp.where(bottom_live, bottom, blocks)] = lower
        return carry

    lax.fori_loop(0, levels, back, 0)
    row = lax.broadcasted_iota(jnp.int32, (columns_total, columns_total), 0)
    column = lax.broadcasted_iota(jnp.int32, (columns_total, columns_total), 1)
    for c in range(members):
        reduced_out[c, 0] = edge[c] + mm(coupled[c].T, solved[c, live[c] - 1])
        flat = solved[c, :blocks].reshape(blocks * width, columns_total)
        inside = lax.broadcasted_iota(jnp.int32, (1, blocks * width), 1) < live[c] * width
        weight = jnp.where(inside, inner_mass[c : c + 1, :], 0.0)
        heavy = flat.T * weight
        diagonal = jnp.where(row == column, edge_mass[c : c + 1, :], 0.0)
        reduced_out[c, 1] = diagonal + mm(heavy, flat)
        coupling_out[c] = mm(jnp.where(inside, modes[c].T, 0.0) * weight, flat)


    parts = len(pieces_out)
    owned = width // parts
    for m in range(parts):
        begin = pl.multiple_of((place[0] ^ m) * owned, owned)
        for c in range(members):
            for kind in range(2):
                for a in range(columns_total // width):
                    pieces_out[m][c, kind, a] = reduced_out[
                        c, kind, pl.ds(a * width + begin, owned), :
                    ]


def reduce_members(counts, place, parts, diag, links, coupled, edge, inner_mass, edge_mass, modes):
    members, blocks, width, _ = diag.shape
    columns_total = coupled.shape[2]
    modes_total = modes.shape[2]
    depth = blocks // 2
    owned = width // parts
    vmem = pl.BlockSpec(memory_space=pltpu.VMEM)
    smem = pl.BlockSpec(memory_space=pltpu.SMEM)
    f32 = jnp.float32
    piece = jax.ShapeDtypeStruct((members, 2, columns_total // width, owned, columns_total), f32)
    return pl.pallas_call(
        reduce_kernel,
        out_shape=(
            jax.ShapeDtypeStruct((members, 2, columns_total, columns_total), f32),
            jax.ShapeDtypeStruct((members, modes_total, columns_total), f32),
        )
        + (piece,) * parts,
        in_specs=[smem, smem] + [vmem] * 7,
        out_specs=(vmem,) * (2 + parts),
        scratch_shapes=[
            pltpu.VMEM((2 * members, width, width), f32),
            pltpu.VMEM((2 * members, width, width), f32),
            pltpu.VMEM((depth, 2 * members, width, width), f32),
            pltpu.VMEM((depth, members, width, columns_total), f32),
            pltpu.VMEM((members, width, columns_total), f32),
            pltpu.VMEM((members, blocks + 1, width, columns_total), f32),
        ],
        cost_estimate=pl.CostEstimate(
            flops=20_000_000_000, bytes_accessed=8_000_000, transcendentals=0
        ),
        name="reduce_members",
    )(counts, place, diag, links, coupled, edge, inner_mass, edge_mass, modes)


def modal_kernel(targets, reduced, modes, local_out):
    members, kinds, columns_total, _ = reduced.shape
    edges = targets.shape[0] // members
    width = columns_total // edges
    for kind in range(kinds):
        total = None
        for c in range(members):
            picked = jnp.concatenate(
                [
                    modes[pl.ds(pl.multiple_of(targets[c * edges + a] * width, width), width), :]
                    for a in range(edges)
                ],
                0,
            )
            part = mm(picked.T, mm(reduced[c, kind], picked))
            total = part if total is None else total + part
        local_out[kind] = total


def modal_share(targets, reduced, modes):
    vmem = pl.BlockSpec(memory_space=pltpu.VMEM)
    width = modes.shape[1]
    return pl.pallas_call(
        modal_kernel,
        out_shape=jax.ShapeDtypeStruct((reduced.shape[1], width, width), jnp.float32),
        in_specs=[pl.BlockSpec(memory_space=pltpu.SMEM), vmem, vmem],
        out_specs=vmem,
        cost_estimate=pl.CostEstimate(
            flops=1_000_000_000, bytes_accessed=2_000_000, transcendentals=0
        ),
        name="modal_share",
    )(targets, reduced, modes)


def gather_kernel(stride, targets, bit, *refs):
    parts = len(refs) - 3
    pieces = refs[:parts]
    keep_out, send_out, total = refs[parts:]
    slots = total.shape[0]
    members, kinds, edges, owned, columns_total = pieces[0].shape
    width = columns_total // edges
    total[...] = jnp.zeros_like(total)
    for m in range(parts):
        for c in range(members):
            where = [targets[(m * members + c) * edges + a] for a in range(edges)]
            for kind in range(kinds):
                for a in range(edges):
                    for b in range(edges):
                        at = pl.ds(pl.multiple_of(where[b] * width, width), width)
                        total[where[a], kind, :, at] += pieces[m][
                            c, kind, a, :, b * width : (b + 1) * width
                        ]
    mine = bit[0]
    for slot in range(slots // 2):
        first = (slot // stride) * 2 * stride + slot % stride
        keep_out[slot] = total[first + mine * stride]
        send_out[slot] = total[first + (1 - mine) * stride]


def gather_rows(targets, bit, stride, pieces, slots):
    members, kinds, edges, owned, columns_total = pieces[0].shape
    full = slots * (columns_total // edges)
    vmem = pl.BlockSpec(memory_space=pltpu.VMEM)
    smem = pl.BlockSpec(memory_space=pltpu.SMEM)
    half = jax.ShapeDtypeStruct((slots // 2, kinds, owned, full), jnp.float32)
    return pl.pallas_call(
        functools.partial(gather_kernel, stride),
        out_shape=(half, half),
        in_specs=[smem, smem] + [vmem] * len(pieces),
        out_specs=(vmem, vmem),
        scratch_shapes=[pltpu.VMEM((slots, kinds, owned, full), jnp.float32)],
        cost_estimate=pl.CostEstimate(
            flops=100_000_000, bytes_accessed=4_000_000, transcendentals=0
        ),
        name="gather_rows",
    )(targets, bit, *pieces)


def on_device(
    interior_stiffness,
    interior_links,
    coupling_stiffness,
    interface_stiffness,
    interior_mass,
    interface_mass,
    interior_modes,
    interior_blocks,
    interface_blocks,
    parent_modes,
):
    cores = lax.axis_size("dev")
    devices = lax.axis_size("grp") * cores
    members, edges = interface_blocks.shape
    per_block = devices // PB
    me = lax.axis_index(AXES)

    def across(value, mask):
        return lax.ppermute(value, AXES, [(d, d ^ mask) for d in range(devices)])

    spread_modes = jnp.broadcast_to(parent_modes[None], (devices,) + parent_modes.shape)
    all_modes = lax.all_to_all(spread_modes, AXES, 0, 0, tiled=True).reshape(
        devices * parent_modes.shape[0], parent_modes.shape[1]
    )
    targets = [interface_blocks.reshape(-1)]
    for m in range(1, per_block):
        targets.append(across(targets[0], m))
    reduced, coupling, *pieces = reduce_members(
        interior_blocks,
        (me % per_block)[None],
        per_block,
        interior_stiffness,
        interior_links,
        coupling_stiffness,
        interface_stiffness,
        interior_mass,
        interface_mass,
        interior_modes,
    )
    arrived = [pieces[0]] + [across(pieces[m], m) for m in range(1, per_block)]
    share = modal_share(targets[0], reduced, all_modes)
    kinds, modes_total, _ = share.shape
    rows = modes_total // devices
    split = share.reshape(kinds, devices, rows, modes_total).transpose(1, 0, 2, 3)
    modal_in = lax.all_to_all(split, AXES, 0, 0, tiled=True)
    modal_rows = modal_in.reshape(devices, kinds, rows, modes_total).sum(0)
    scaling = (PB / (members * devices * edges)) ** 0.5
    modal_rows = modal_rows * scaling
    modal_all = lax.all_to_all(
        jnp.broadcast_to(modal_rows[None], (devices,) + modal_rows.shape), AXES, 0, 0, tiled=True
    )
    modal = modal_all.transpose(1, 0, 2, 3).reshape(kinds, modes_total, modes_total)

    strides = [per_block << k for k in range(PB.bit_length() - 1)]
    order = sorted(strides, key=lambda stride: (stride != cores, -stride))
    bits = {stride: (me // stride) % 2 for stride in strides}
    first = order[0]
    keep, send = gather_rows(
        jnp.concatenate(targets), bits[first][None], first // per_block, arrived, PB
    )
    remaining = sorted(strides, reverse=True)
    remaining.remove(first)
    tail = keep.shape[1:]
    keep = keep.reshape((2,) * len(remaining) + tail)
    got = across(send, first).reshape(keep.shape)
    for stride in order[1:]:
        axis = remaining.index(stride)
        remaining.remove(stride)
        bit = bits[stride]

        def pick(which):
            return lax.dynamic_index_in_dim(keep, which, axis, False) + lax.dynamic_index_in_dim(
                got, which, axis, False
            )

        send = pick(1 - bit)
        got_next = across(send, stride)
        keep, got = pick(bit), got_next
    total = (keep + got) * scaling
    return (total[0], total[1], coupling, modal[0], modal[1])


def solution(mesh):
    placed = (
        P(AXES, None, None, None),
        P(AXES, None, None, None),
        P(AXES, None, None),
        P(AXES, None, None),
        P(AXES, None),
        P(AXES, None),
        P(AXES, None, None),
        P(AXES),
        P(AXES, None),
        P(AXES, None),
    )
    return jax.shard_map(
        on_device,
        mesh=mesh,
        in_specs=placed,
        out_specs=(P(AXES, None), P(AXES, None), P(AXES, None, None), P(), P()),
        check_vma=False,
    )
```

time: 906 us -> 145 us (0.16)
  other arithmetic: 549 us -> 1.69 us
  waiting for transfers between devices: 229 us -> 42.9 us
  Pallas kernels: 0 us -> 50.5 us
  matrix products: 42.4 us -> 0 us
  local copies, waits for them, and re-layouts: 35 us -> 8.11 us
  starting transfers between devices: 16.7 us -> 38.8 us
  loops' own time: 17.7 us -> 0 us
  between operations: 14.2 us -> 0.83 us
    another operation x123 -> x0, other arithmetic: 533 us -> none  [the longest x48 199 us: eliminate_advance(): factor = jnp.linalg.cholesky(schur_part)]
    psum x1 -> x0, waiting for transfers between devices: 130 us -> none  [on_device(): lax.psum((local_stiff, local_mass), ('grp', 'dev'))]
    all_to_all x3, waiting for transfers between devices: 94.7 us -> 13.4 us  [the longest x1 13.4 us: on_device(): modal_in = lax.all_to_all(split, AXES, 0, 0, tiled=True)]
    pallas_call x0 -> x3, Pallas kernels: none -> 50.5 us  [the longest x1 42.3 us: reduce_members(): pl.pallas_call(reduce_kernel, out_shape=(jax.ShapeDtypeStruct((members, 2...]
    dot_general x46 -> x0, matrix products: 34.2 us -> none  [the longest x42 24.4 us: product(): jnp.dot(left, right, precision=lax.Precision.HIGHEST, preferred_element_t...]
    ppermute x0 -> x9, waiting for transfers between devices: none -> 29.5 us  [across(): return lax.ppermute(value, AXES, [(d, d ^ mask) for d in range(devices)])]
    ppermute x0 -> x9, starting transfers between devices: none -> 19.4 us  [across(): return lax.ppermute(value, AXES, [(d, d ^ mask) for d in range(devices)])]
    another operation x5 -> x0, loops' own time: 17.7 us -> none  [the longest x2 11.9 us: solve_padded(): lax.scan(solve_advance, jnp.zeros_like(forward), (factors, ahead_links, p...]
  transfers between devices with their start and end apart: 5 -> 12, of which waited for: 4 -> 5; matrix products, arithmetic and copies ran while one was open for 68% -> 4% of each run, Pallas kernels for 0% -> 35%
where the time goes in v1:
time: 145 us; the launch traced here: 143 us
  Pallas kernels  50.5 us (35%)
  waiting for transfers between devices  42.9 us (30%)
  starting transfers between devices  38.8 us (27%)
  local copies, waits for them, and re-layouts  8.11 us (6%)
  other arithmetic  1.69 us (1%)
    pallas_call x1, Pallas kernels, reduce_members(): pl.pallas_call(reduce_kernel, out_shape=(jax.ShapeDtypeStruct((members, 2...  42.3 us
    ppermute x9, waiting for transfers between devices, across(): return lax.ppermute(value, AXES, [(d, d ^ mask) for d in range(devices)])  29.5 us
    ppermute x9, starting transfers between devices, across(): return lax.ppermute(value, AXES, [(d, d ^ mask) for d in range(devices)])  19.4 us
    all_to_all x1, waiting for transfers between devices, on_device(): modal_in = lax.all_to_all(split, AXES, 0, 0, tiled=True)  13.4 us
    all_to_all x1, starting transfers between devices, on_device(): modal_in = lax.all_to_all(split, AXES, 0, 0, tiled=True)  9.47 us
    all_to_all x1, starting transfers between devices, on_device(): lax.all_to_all(spread_modes, AXES, 0, 0, tiled=True)  7.33 us
    pallas_call x1, Pallas kernels, modal_share(): pl.pallas_call(modal_kernel, out_shape=jax.ShapeDtypeStruct((reduced.shap...  5.16 us
    pallas_call x1, Pallas kernels, gather_rows(): pl.pallas_call(functools.partial(gather_kernel, stride), out_shape=(half,...  3.05 us
  transfers between devices with their start and end apart: 12, of which 5 were waited for; matrix products, arithmetic and copies ran while one was open for 4% of the time, Pallas kernels for 35%

profile of v1, /device:TPU:0, one launch (start us, length us, event | category | flops | bytes accessed | tf_op | source)
XLA Modules:
  0.0 142.8 jit_solution(6675239842777042508)
XLA Ops:
  0.6 1.8 %broadcast_in_dim.20 = f32[32,32,256]{2,1,0:T(8,128)} broadcast(f32[32,256]{1,0:T(8,128)} %param.19), dimensions={1,2} | broadcast | bytes 1081344 | tf_op jit(solution)/shard_map/broadcast_in_dim | solution.py:308
  2.5 7.3 %all-to-all-start = ((f32[32,32,256]{2,1,0:T(8,128)}), f32[32,32,256]{2,1,0:T(8,128)S(1)}, u32[]{:S(2)}, u32[]{:S(2)}) async-start(f32[32,32,256]{2,1,0:T(8,128)} %broadcast_in_dim.20), calls=%async_computation | async-start | bytes 2097152 | tf_op jit(solution)/shard_map/all_to_all | solution.py:309
  9.8 0.0 copy-start.6
  9.8 42.3 %reduce_members.1 = (f32[2,2,256,256]{3,2,1,0:T(8,128)}, f32[2,256,256]{2,1,0:T(8,128)}, f32[2,2,2,32,256]{4,3,2,1,0:T(8,128)}, f32[2,2,2,32,256]{4,3,2,1,0:T(8,...) custom-call(s32[2]{0:T(128)} %counts.1, s32[1]{0:T(128)} %bitcast.1.place, f32[2,8,128,128]{3,2,1,0:T(8,128)} %diag.1, ...), custom_call_target="tpu_custom_call" | custom-call | flops 20000000000 | bytes 8000000 | tf_op jit(solution)/shard_map/reduce_members/pallas_call | solution.py:185
  52.1 1.8 %collective-permute-start.3 = (f32[2,2,2,32,256]{4,3,2,1,0:T(8,128)}, f32[2,2,2,32,256]{4,3,2,1,0:T(8,128)S(1)}, u32[]{:S(2)}, u32[]{:S(2)}) collective-permute-start(f32[2,2,2,32,256]{4,3,2,1,0:T(8,128)} %get-tuple-element.14), channel_id=1, source_target_pairs={{0,1},{1,0},{2,3},{3,2},{4,5},{5,4},{6,7},{7,6},{8,9},{9,8},{10,11... | collective-permute-start | bytes 786440 | tf_op jit(solution)/shard_map/ppermute | solution.py:306
  53.9 1.5 %collective-permute-start.4 = (f32[2,2,2,32,256]{4,3,2,1,0:T(8,128)}, f32[2,2,2,32,256]{4,3,2,1,0:T(8,128)S(1)}, u32[]{:S(2)}, u32[]{:S(2)}) collective-permute-start(f32[2,2,2,32,256]{4,3,2,1,0:T(8,128)} %get-tuple-element.15), channel_id=1, source_target_pairs={{0,2},{1,3},{2,0},{3,1},{4,6},{5,7},{6,4},{7,5},{8,10},{9,11},{10,... | collective-permute-start | bytes 786440 | tf_op jit(solution)/shard_map/ppermute | solution.py:306
  55.3 0.3 collective-permute-start.5
  55.6 0.0 copy-done.6
  55.6 0.1 reshape.40.targets
  55.7 0.0 copy-start.5
  55.7 2.7 %collective-permute-start.2 = (s32[4]{0:T(128)S(1)}, s32[4]{0:T(128)S(1)}, u32[]{:S(2)}, u32[]{:S(2)}) collective-permute-start(s32[4]{0:T(128)S(1)} %reshape.40.targets), channel_id=1, source_target_pairs={{0,3},{1,2},{2,1},{3,0},{4,7},{5,6},{6,5},{7,4},{8,11},{9,10},{10,... | collective-permute-start | bytes 56 | tf_op jit(solution)/shard_map/ppermute | solution.py:306
  58.4 0.6 collective-permute-start.1
  58.9 4.1 %collective-permute-done.2 = s32[4]{0:T(128)S(1)} collective-permute-done((s32[4]{0:T(128)S(1)}, s32[4]{0:T(128)S(1)}, u32[]{:S(2)}, u32[]{:S(2)}) %collective-permute-start.2) | collective-permute-done | bytes 48 | tf_op jit(solution)/shard_map/ppermute | solution.py:306
  63.1 1.8 %collective-permute-start = (s32[4]{0:T(128)S(1)}, s32[4]{0:T(128)S(1)}, u32[]{:S(2)}, u32[]{:S(2)}) collective-permute-start(s32[4]{0:T(128)S(1)} %reshape.40.targets), channel_id=1, source_target_pairs={{0,1},{1,0},{2,3},{3,2},{4,5},{5,4},{6,7},{7,6},{8,9},{9,8},{10,11... | collective-permute-start | bytes 56 | tf_op jit(solution)/shard_map/ppermute | solution.py:306
  64.8 0.0 collective-permute-done.1
  64.8 1.8 %collective-permute-done = s32[4]{0:T(128)S(1)} collective-permute-done((s32[4]{0:T(128)S(1)}, s32[4]{0:T(128)S(1)}, u32[]{:S(2)}, u32[]{:S(2)}) %collective-permute-start) | collective-permute-done | bytes 48 | tf_op jit(solution)/shard_map/ppermute | solution.py:306
  66.6 0.6 pad_add_fusion.targets
  67.2 0.0 collective-permute-done.3.refs_1_
  67.2 0.0 copy-start.2
  67.2 0.0 collective-permute-done.4.refs_2_
  67.2 0.0 copy-start.3
  67.2 0.0 collective-permute-done.5.refs_3_
  67.3 0.0 copy-start.4
  67.3 0.7 copy-done.2
  67.9 0.1 copy-done.3
  68.0 0.1 copy-done.4
  68.1 3.1 %gather_rows.1 = (f32[4,2,32,1024]{3,2,1,0:T(8,128)}, f32[4,2,32,1024]{3,2,1,0:T(8,128)}) custom-call(s32[16]{0:T(128)} %pad_add_fusion.targets, s32[1]{0:T(128)} %bitcast.bit, f32[2,2,2,32,256]{4,3,2,1,0:T(8,128)} %get-tuple-element.13.refs_0_, f32[2,2,2,32,256]{4,3,2,1,0:T(8,128)} %copy-done.2, f32[2,2,2,32,256]{4,3,2,1,0:T(8,128)} %copy-done.3, ...), custom_call_target="tpu_custom_call" | custom-call | flops 100000000 | bytes 4000000 | tf_op jit(solution)/shard_map/gather_rows/pallas_call | solution.py:274
  71.2 6.5 %collective-permute-start.6 = (f32[4,2,32,1024]{3,2,1,0:T(8,128)}, f32[4,2,32,1024]{3,2,1,0:T(8,128)S(1)}, u32[]{:S(2)}, u32[]{:S(2)}) collective-permute-start(f32[4,2,32,1024]{3,2,1,0:T(8,128)} %get-tuple-element.18), channel_id=1, source_target_pairs={{0,8},{1,9},{2,10},{3,11},{4,12},{5,13},{6,14},{7,15},{8,0},{9,1},... | collective-permute-start | bytes 3145736 | tf_op jit(solution)/shard_map/ppermute | solution.py:306
  77.7 0.0 all-to-all-done
  77.7 0.0 copy-start
  77.7 0.0 copy-done.5
  77.7 1.0 copy-done
  78.7 0.0 copy-start.1
  78.7 5.2 %modal_share.1 = f32[2,256,256]{2,1,0:T(8,128)} custom-call(s32[4]{0:T(128)} %copy-done.5, f32[2,2,256,256]{3,2,1,0:T(8,128)} %get-tuple-element.20.reduced, f32[1024,256]{1,0:T(8,128)} %bitcast.36), custom_call_target="tpu_custom_call" | custom-call | flops 1000000000 | bytes 2000000 | tf_op jit(solution)/shard_map/modal_share/pallas_call | solution.py:231
  83.8 1.9 %copy_bitcast_fusion = f32[32,2,8,256]{3,2,1,0:T(8,128)} fusion(f32[2,256,256]{2,1,0:T(8,128)} %modal_share.1), kind=kLoop, calls=%fused_computation | loop fusion | bytes 1048576 | tf_op jit(solution)/shard_map/transpose | solution.py:331
  85.7 9.5 %all-to-all-start.1 = ((f32[32,2,8,256]{3,2,1,0:T(8,128)}), f32[32,2,8,256]{3,2,1,0:T(8,128)S(1)}, u32[]{:S(2)}, u32[]{:S(2)}) async-start(f32[32,2,8,256]{3,2,1,0:T(8,128)} %copy_bitcast_fusion), calls=%async_computation.1 | async-start | bytes 1048576 | tf_op jit(solution)/shard_map/all_to_all | solution.py:332
  95.3 0.0 collective-permute-done.6
  95.3 0.0 copy-done.1
  95.3 1.0 dynamic-slice_add_fusion
  96.3 1.8 %collective-permute-start.7 = (f32[2,2,32,1024]{3,2,1,0:T(8,128)}, f32[2,2,32,1024]{3,2,1,0:T(8,128)S(1)}, u32[]{:S(2)}, u32[]{:S(2)}) collective-permute-start(f32[2,2,32,1024]{3,2,1,0:T(8,128)} %get-tuple-element.22), channel_id=1, source_target_pairs={{0,16},{1,17},{2,18},{3,19},{4,20},{5,21},{6,22},{7,23},{8,24},{9,... | collective-permute-start | bytes 1572872 | tf_op jit(solution)/shard_map/ppermute | solution.py:306
  98.0 13.4 %all-to-all-done.1 = f32[32,2,8,256]{3,2,1,0:T(8,128)S(1)} async-done(((f32[32,2,8,256]{3,2,1,0:T(8,128)}), f32[32,2,8,256]{3,2,1,0:T(8,128)S(1)}, u32[]{:S(2)}, u32[]{:S(2)}) %all-to-all-start.1) | async-done | bytes 524320 | tf_op jit(solution)/shard_map/all_to_all | solution.py:332
  111.5 0.9 broadcast_in_dim.21
  112.4 2.6 %all-to-all-start.2 = ((f32[32,2,8,256]{3,2,1,0:T(8,128)}), f32[32,2,8,256]{3,2,1,0:T(8,128)S(1)}, u32[]{:S(2)}, u32[]{:S(2)}) async-start(f32[32,2,8,256]{3,2,1,0:T(8,128)} %broadcast_in_dim.21), calls=%async_computation.2 | async-start | bytes 1048576 | tf_op jit(solution)/shard_map/all_to_all | solution.py:336
  115.0 0.1 collective-permute-done.7
  115.2 2.6 %collective-permute-start.8 = (f32[2,32,1024]{2,1,0:T(8,128)S(1)}, f32[2,32,1024]{2,1,0:T(8,128)S(1)}, u32[]{:S(2)}, u32[]{:S(2)}) collective-permute-start(f32[2,32,1024]{2,1,0:T(8,128)S(1)} %fusion), channel_id=1, source_target_pairs={{0,4},{1,5},{2,6},{3,7},{4,0},{5,1},{6,2},{7,3},{8,12},{9,13},{10,... | collective-permute-start | bytes 786440 | tf_op jit(solution)/shard_map/ppermute | solution.py:306
  117.8 23.4 %collective-permute-done.8 = f32[2,32,1024]{2,1,0:T(8,128)S(1)} collective-permute-done((f32[2,32,1024]{2,1,0:T(8,128)S(1)}, f32[2,32,1024]{2,1,0:T(8,128)S(1)}, u32[]{:S(2)}, u32[]{:S(2)}) %collective-permute-start.8) | collective-permute-done | bytes 262176 | tf_op jit(solution)/shard_map/ppermute | solution.py:306
  141.2 0.7 slice_bitcast_fusion.2
  142.0 0.0 all-to-all-done.2
  142.0 0.8 slice_bitcast_fusion
  (4 shorter events, 0.1 us)
Async XLA Ops:
  2.5 75.2 %all-to-all-start = ((f32[32,32,256]{2,1,0:T(8,128)}), f32[32,32,256]{2,1,0:T(8,128)S(1)}, u32[]{:S(2)}, u32[]{:S(2)}) async-start(f32[32,32,256]{2,1,0:T(8,128)} %broadcast_in_dim.20), calls=%async_computation | async-start | bytes 2097152 | tf_op jit(solution)/shard_map/all_to_all | solution.py:309
  9.8 45.8 %copy-start.6 = (s32[2,2]{1,0:T(2,128)S(1)}, s32[2,2]{1,0:T(2,128)}, u32[]{:S(2)}) copy-start(s32[2,2]{1,0:T(2,128)} %param.18) | copy-start | bytes 52
  52.1 15.1 %collective-permute-start.3 = (f32[2,2,2,32,256]{4,3,2,1,0:T(8,128)}, f32[2,2,2,32,256]{4,3,2,1,0:T(8,128)S(1)}, u32[]{:S(2)}, u32[]{:S(2)}) collective-permute-start(f32[2,2,2,32,256]{4,3,2,1,0:T(8,128)} %get-tuple-element.14), channel_id=1, source_target_pairs={{0,1},{1,0},{2,3},{3,2},{4,5},{5,4},{6,7},{7,6},{8,9},{9,8},{10,11... | collective-permute-start | bytes 786440 | tf_op jit(solution)/shard_map/ppermute | solution.py:306
  53.9 13.3 %collective-permute-start.4 = (f32[2,2,2,32,256]{4,3,2,1,0:T(8,128)}, f32[2,2,2,32,256]{4,3,2,1,0:T(8,128)S(1)}, u32[]{:S(2)}, u32[]{:S(2)}) collective-permute-start(f32[2,2,2,32,256]{4,3,2,1,0:T(8,128)} %get-tuple-element.15), channel_id=1, source_target_pairs={{0,2},{1,3},{2,0},{3,1},{4,6},{5,7},{6,4},{7,5},{8,10},{9,11},{10,... | collective-permute-start | bytes 786440 | tf_op jit(solution)/shard_map/ppermute | solution.py:306
  55.3 11.9 %collective-permute-start.5 = (f32[2,2,2,32,256]{4,3,2,1,0:T(8,128)}, f32[2,2,2,32,256]{4,3,2,1,0:T(8,128)S(1)}, u32[]{:S(2)}, u32[]{:S(2)}) collective-permute-start(f32[2,2,2,32,256]{4,3,2,1,0:T(8,128)} %get-tuple-element.16), channel_id=1, source_target_pairs={{0,3},{1,2},{2,1},{3,0},{4,7},{5,6},{6,5},{7,4},{8,11},{9,10},{10,... | collective-permute-start | bytes 786440 | tf_op jit(solution)/shard_map/ppermute | solution.py:306
  55.7 22.0 %copy-start.5 = (s32[4]{0:T(128)}, s32[4]{0:T(128)S(1)}, u32[]{:S(2)}) copy-start(s32[4]{0:T(128)S(1)} %reshape.40.targets) | copy-start | bytes 52
  55.7 7.4 %collective-permute-start.2 = (s32[4]{0:T(128)S(1)}, s32[4]{0:T(128)S(1)}, u32[]{:S(2)}, u32[]{:S(2)}) collective-permute-start(s32[4]{0:T(128)S(1)} %reshape.40.targets), channel_id=1, source_target_pairs={{0,3},{1,2},{2,1},{3,0},{4,7},{5,6},{6,5},{7,4},{8,11},{9,10},{10,... | collective-permute-start | bytes 56 | tf_op jit(solution)/shard_map/ppermute | solution.py:306
  58.4 6.5 %collective-permute-start.1 = (s32[4]{0:T(128)S(1)}, s32[4]{0:T(128)S(1)}, u32[]{:S(2)}, u32[]{:S(2)}) collective-permute-start(s32[4]{0:T(128)S(1)} %reshape.40.targets), channel_id=1, source_target_pairs={{0,2},{1,3},{2,0},{3,1},{4,6},{5,7},{6,4},{7,5},{8,10},{9,11},{10,... | collective-permute-start | bytes 56 | tf_op jit(solution)/shard_map/ppermute | solution.py:306
  63.1 3.6 %collective-permute-start = (s32[4]{0:T(128)S(1)}, s32[4]{0:T(128)S(1)}, u32[]{:S(2)}, u32[]{:S(2)}) collective-permute-start(s32[4]{0:T(128)S(1)} %reshape.40.targets), channel_id=1, source_target_pairs={{0,1},{1,0},{2,3},{3,2},{4,5},{5,4},{6,7},{7,6},{8,9},{9,8},{10,11... | collective-permute-start | bytes 56 | tf_op jit(solution)/shard_map/ppermute | solution.py:306
  67.2 0.7 copy-start.2
  67.2 0.8 copy-start.3
  67.3 0.9 copy-start.4
  71.2 24.1 %collective-permute-start.6 = (f32[4,2,32,1024]{3,2,1,0:T(8,128)}, f32[4,2,32,1024]{3,2,1,0:T(8,128)S(1)}, u32[]{:S(2)}, u32[]{:S(2)}) collective-permute-start(f32[4,2,32,1024]{3,2,1,0:T(8,128)} %get-tuple-element.18), channel_id=1, source_target_pairs={{0,8},{1,9},{2,10},{3,11},{4,12},{5,13},{6,14},{7,15},{8,0},{9,1},... | collective-permute-start | bytes 3145736 | tf_op jit(solution)/shard_map/ppermute | solution.py:306
  77.7 1.0 copy-start
  78.7 16.6 %copy-start.1 = (f32[4,2,32,1024]{3,2,1,0:T(8,128)S(1)}, f32[4,2,32,1024]{3,2,1,0:T(8,128)}, u32[]{:S(2)}) copy-start(f32[4,2,32,1024]{3,2,1,0:T(8,128)} %get-tuple-element.17) | copy-start | bytes 3145732
  85.7 25.7 %all-to-all-start.1 = ((f32[32,2,8,256]{3,2,1,0:T(8,128)}), f32[32,2,8,256]{3,2,1,0:T(8,128)S(1)}, u32[]{:S(2)}, u32[]{:S(2)}) async-start(f32[32,2,8,256]{3,2,1,0:T(8,128)} %copy_bitcast_fusion), calls=%async_computation.1 | async-start | bytes 1048576 | tf_op jit(solution)/shard_map/all_to_all | solution.py:332
  96.3 18.9 %collective-permute-start.7 = (f32[2,2,32,1024]{3,2,1,0:T(8,128)}, f32[2,2,32,1024]{3,2,1,0:T(8,128)S(1)}, u32[]{:S(2)}, u32[]{:S(2)}) collective-permute-start(f32[2,2,32,1024]{3,2,1,0:T(8,128)} %get-tuple-element.22), channel_id=1, source_target_pairs={{0,16},{1,17},{2,18},{3,19},{4,20},{5,21},{6,22},{7,23},{8,24},{9,... | collective-permute-start | bytes 1572872 | tf_op jit(solution)/shard_map/ppermute | solution.py:306
  112.4 29.6 %all-to-all-start.2 = ((f32[32,2,8,256]{3,2,1,0:T(8,128)}), f32[32,2,8,256]{3,2,1,0:T(8,128)S(1)}, u32[]{:S(2)}, u32[]{:S(2)}) async-start(f32[32,2,8,256]{3,2,1,0:T(8,128)} %broadcast_in_dim.21), calls=%async_computation.2 | async-start | bytes 1048576 | tf_op jit(solution)/shard_map/all_to_all | solution.py:336
  115.2 26.0 %collective-permute-start.8 = (f32[2,32,1024]{2,1,0:T(8,128)S(1)}, f32[2,32,1024]{2,1,0:T(8,128)S(1)}, u32[]{:S(2)}, u32[]{:S(2)}) collective-permute-start(f32[2,32,1024]{2,1,0:T(8,128)S(1)} %fusion), channel_id=1, source_target_pairs={{0,4},{1,5},{2,6},{3,7},{4,0},{5,1},{6,2},{7,3},{8,12},{9,13},{10,... | collective-permute-start | bytes 786440 | tf_op jit(solution)/shard_map/ppermute | solution.py:306

commit v2 on v1

v2 whole, which is shorter than its diff:
```python
import functools
import jax
import jax.numpy as jnp
from jax import lax
from jax.experimental import pallas as pl
from jax.experimental.pallas import tpu as pltpu
from jax.sharding import PartitionSpec as P


AXES = ("grp", "dev")
PB = 8

PANEL = 16


def dot(left, right):
    return lax.dot_general(
        left, right, (((1,), (0,)), ((), ())), preferred_element_type=jnp.float32
    )


def mm_high(left, right):
    return lax.dot_general(
        left, right, (((1,), (0,)), ((), ())),
        precision=lax.Precision.HIGH, preferred_element_type=jnp.float32,
    )


def split(value):
    high = value.astype(jnp.bfloat16)
    rest = value - high.astype(jnp.float32)
    middle = rest.astype(jnp.bfloat16)
    low = (rest - middle.astype(jnp.float32)).astype(jnp.bfloat16)
    return high, middle, low


def mm(left, right):
    columns = right.shape[1]
    left_high, left_middle, left_low = split(left)
    high, middle, low = split(right)
    near = jnp.concatenate([left_high, left_middle], 1)
    far = jnp.concatenate([left_high, left_low], 1)
    small = dot(far, jnp.concatenate([low, high], 0))
    if columns <= left.shape[1]:
        both = dot(near, jnp.concatenate([jnp.concatenate([high, middle], 1)] * 2, 0))
        return (small + both[:, columns:]) + both[:, :columns]
    return (small + dot(near, jnp.concatenate([middle] * 2, 0))) + dot(
        near, jnp.concatenate([high] * 2, 0)
    )


def sweep(work, chains, width):
    total = width // PANEL
    panels = [work[g, pl.ds(0, PANEL), :] for g in range(chains)]
    for index in range(total):
        panels = sweep_panel(work, panels, chains, width, index)


def sweep_panel(work, panels, chains, width, index):
    start = index * PANEL
    lane = lax.broadcasted_iota(jnp.int32, (PANEL, width), 1)
    sub = lax.broadcasted_iota(jnp.int32, (PANEL, width), 0)
    chain_of = (lane // PANEL) % chains
    columns = []
    for j in range(PANEL):
        packed = None
        for g in range(chains):
            column = jnp.broadcast_to(panels[g][:, start + j : start + j + 1], (PANEL, width))
            packed = column if packed is None else jnp.where(chain_of == g, column, packed)
        columns.append(packed)
    turned = []
    weights_high, weights_middle, weights_low = [], [], []
    mine = lane // PANEL == index
    unit = jnp.where(lane - start == sub, -1.0, 0.0)
    for g in range(chains):
        high, middle, low = split(panels[g])
        turned.append(jnp.concatenate([high, high, high, middle, middle, low], 0).T)
        high, middle, low = split(jnp.where(mine, unit, panels[g]))
        weights_high.append(high)
        weights_middle.append(middle)
        weights_low.append(low)
    for s in range(PANEL):
        here = columns[s]
        inverse = 1.0 / here[s : s + 1, :]
        scaled = here * inverse
        lowered = jnp.where(sub == s, here - 1.0, here)
        for j in range(PANEL):
            if j != s:
                columns[j] = columns[j] - lowered * scaled[j : j + 1, :]
        columns[s] = jnp.where(sub == s, -inverse, scaled)
    compact = columns[0]
    for j in range(1, PANEL):
        compact = jnp.where(lane % PANEL == j, columns[j], compact)
    group = lane // PANEL
    front = lane < chains * PANEL
    high, middle, low = split(compact)
    high, middle, low = (part.astype(jnp.float32) for part in (high, middle, low))
    front_back = [jnp.where(front, high, middle), jnp.where(front, low, high)]
    stacked = [
        jnp.concatenate(
            [
                jnp.where((group % chains == g) & (group < 2 * chains), part, 0.0)
                for g in range(chains)
            ],
            0,
        ).astype(jnp.bfloat16)
        for part in front_back
    ]
    fill = width - 2 * chains * PANEL
    blank = [jnp.zeros((fill, width), jnp.bfloat16)] if fill > 0 else []
    reduced = dot(stacked[1], jnp.concatenate(weights_high + weights_low + blank, 0))
    reduced = reduced + dot(stacked[0], jnp.concatenate(weights_middle * 2 + blank, 0))
    reduced = reduced + dot(stacked[0], jnp.concatenate(weights_high * 2 + blank, 0))
    after = start + PANEL
    last = after == width
    parts = [reduced[g * PANEL : (g + 1) * PANEL] for g in range(chains)]
    stacks = []
    for g in range(chains):
        high, middle, low = split(parts[g])
        stacks.append(jnp.concatenate([high, middle, low, high, middle, high], 0))
    following = []
    if not last:
        for g in range(chains):
            change = dot(turned[g][after : after + PANEL], stacks[g])
            kept = jnp.where(mine, 0.0, work[g, pl.ds(after, PANEL), :])
            following.append(kept + change)
    for g in range(chains):
        if start > 0:
            here = jnp.where(
                lax.broadcasted_iota(jnp.int32, (start, width), 1) // PANEL == index,
                0.0,
                work[g, :start, :],
            )
            work[g, :start, :] = here + dot(turned[g][:start], stacks[g])
        rest = after + PANEL
        if rest < width:
            here = jnp.where(
                lax.broadcasted_iota(jnp.int32, (width - rest, width), 1) // PANEL == index,
                0.0,
                work[g, rest:, :],
            )
            work[g, rest:, :] = here + dot(turned[g][rest:], stacks[g])
        work[g, pl.ds(start, PANEL), :] = -parts[g]
    return following


def reduce_kernel(
    counts, place, diag, links, coupled, edge, inner_mass, edge_mass, modes,
    reduced_out, coupling_out, *rest,
):
    pieces_out = rest[:-6]
    work, state, moved, ahead, source, solved = rest[-6:]
    members, blocks, width, _ = diag.shape
    chains = 2 * members
    columns_total = coupled.shape[2]
    live = [counts[c] for c in range(members)]
    middle = [live[c] // 2 for c in range(members)]
    below = [live[c] - 1 - middle[c] for c in range(members)]
    levels = middle[0]
    for c in range(1, members):
        levels = jnp.maximum(levels, middle[c])
    for c in range(members):
        work[2 * c] = diag[c, 0]
        state[2 * c] = diag[c, 0]
        work[2 * c + 1] = diag[c, live[c] - 1]
        state[2 * c + 1] = diag[c, live[c] - 1]
        source[c] = coupled[c]
        solved[c] = jnp.zeros(solved.shape[1:], jnp.float32)

    def level(t, carry):
        sweep(work, chains, width)
        last = t == levels - 1
        for c in range(members):
            top = jnp.minimum(t, blocks - 2)
            top_after = jnp.minimum(t + 1, blocks - 1)
            bottom = jnp.maximum(live[c] - 2 - t, 0)
            link_top = links[c, top]
            link_bottom = links[c, bottom]
            top_work, bottom_work = work[2 * c], work[2 * c + 1]
            moved_top = mm(top_work, link_top.T)
            moved_bottom = mm(bottom_work, link_bottom)
            ahead_now = mm(bottom_work, source[c])
            moved[t, 2 * c] = moved_top
            moved[t, 2 * c + 1] = moved_bottom
            ahead[t, c] = ahead_now
            link_turned = link_bottom.T
            next_top = diag[c, top_after] + mm(link_top, moved_top)
            next_bottom = diag[c, bottom] + mm(link_turned, moved_bottom)
            next_source = mm(link_turned, ahead_now)
            next_top = jnp.where(t < middle[c], next_top, state[2 * c])
            next_bottom = jnp.where(t < below[c], next_bottom, state[2 * c + 1])
            source[c] = jnp.where(t < below[c], next_source, source[c])
            state[2 * c] = next_top
            state[2 * c + 1] = next_bottom
            work[2 * c] = next_top
            work[2 * c + 1] = next_bottom

        @pl.when(last)
        def _():
            for c in range(members):
                joined = state[2 * c] - (diag[c, middle[c]] - state[2 * c + 1])
                work[c] = joined

        return carry

    lax.fori_loop(0, levels, level, 0)
    sweep(work, members, width)
    for c in range(members):
        solved[c, middle[c]] = mm(work[c], source[c])

    def back(s, carry):
        for c in range(members):
            top = middle[c] - 1 - s
            top_live = top >= 0
            top_safe = jnp.maximum(top, 0)
            upper = mm(moved[top_safe, 2 * c], solved[c, top_safe + 1])
            bottom = middle[c] + 1 + s
            bottom_live = bottom < live[c]
            bottom_safe = jnp.where(bottom_live, bottom, 1)
            step = jnp.where(bottom_live, live[c] - 1 - bottom, 0)
            lower = ahead[step, c] + mm(moved[step, 2 * c + 1], solved[c, bottom_safe - 1])
            solved[c, jnp.where(top_live, top, blocks)] = upper
            solved[c, jnp.where(bottom_live, bottom, blocks)] = lower
        return carry

    lax.fori_loop(0, levels, back, 0)
    row = lax.broadcasted_iota(jnp.int32, (columns_total, columns_total), 0)
    column = lax.broadcasted_iota(jnp.int32, (columns_total, columns_total), 1)
    for c in range(members):
        reduced_out[c, 0] = edge[c] + mm_high(coupled[c].T, solved[c, live[c] - 1])
        flat = solved[c, :blocks].reshape(blocks * width, columns_total)
        inside = lax.broadcasted_iota(jnp.int32, (1, blocks * width), 1) < live[c] * width
        weight = jnp.where(inside, inner_mass[c : c + 1, :], 0.0)
        heavy = flat.T * weight
        diagonal = jnp.where(row == column, edge_mass[c : c + 1, :], 0.0)
        reduced_out[c, 1] = diagonal + mm_high(heavy, flat)
        coupling_out[c] = mm_high(jnp.where(inside, modes[c].T, 0.0) * weight, flat)


    parts = len(pieces_out)
    owned = width // parts
    for m in range(parts):
        begin = pl.multiple_of((place[0] ^ m) * owned, owned)
        for c in range(members):
            for kind in range(2):
                for a in range(columns_total // width):
                    pieces_out[m][c, kind, a] = reduced_out[
                        c, kind, pl.ds(a * width + begin, owned), :
                    ]


def reduce_members(counts, place, parts, diag, links, coupled, edge, inner_mass, edge_mass, modes):
    members, blocks, width, _ = diag.shape
    columns_total = coupled.shape[2]
    modes_total = modes.shape[2]
    depth = blocks // 2
    owned = width // parts
    vmem = pl.BlockSpec(memory_space=pltpu.VMEM)
    smem = pl.BlockSpec(memory_space=pltpu.SMEM)
    f32 = jnp.float32
    piece = jax.ShapeDtypeStruct((members, 2, columns_total // width, owned, columns_total), f32)
    return pl.pallas_call(
        reduce_kernel,
        out_shape=(
            jax.ShapeDtypeStruct((members, 2, columns_total, columns_total), f32),
            jax.ShapeDtypeStruct((members, modes_total, columns_total), f32),
        )
        + (piece,) * parts,
        in_specs=[smem, smem] + [vmem] * 7,
        out_specs=(vmem,) * (2 + parts),
        scratch_shapes=[
            pltpu.VMEM((2 * members, width, width), f32),
            pltpu.VMEM((2 * members, width, width), f32),
            pltpu.VMEM((depth, 2 * members, width, width), f32),
            pltpu.VMEM((depth, members, width, columns_total), f32),
            pltpu.VMEM((members, width, columns_total), f32),
            pltpu.VMEM((members, blocks + 1, width, columns_total), f32),
        ],
        cost_estimate=pl.CostEstimate(
            flops=20_000_000_000, bytes_accessed=8_000_000, transcendentals=0
        ),
        compiler_params=pltpu.CompilerParams(vmem_limit_bytes=24 * 1024 * 1024),
        name="reduce_members",
    )(counts, place, diag, links, coupled, edge, inner_mass, edge_mass, modes)


def spread_kernel(targets, modes, out):
    devices, rows, width = out.shape
    owned = modes.shape[0]
    lane = lax.broadcasted_iota(jnp.int32, (rows - owned, width), 1)
    named = jnp.zeros((rows - owned, width), jnp.int32)
    members, edges = targets.shape
    for k in range(members * edges):
        named = jnp.where(lane == k, targets[k // edges, k % edges], named)
    whole = jnp.concatenate([modes[...], named.astype(jnp.float32)], 0)
    for d in range(devices):
        out[d] = whole


def spread_modes(targets, modes, devices):
    vmem = pl.BlockSpec(memory_space=pltpu.VMEM)
    owned, width = modes.shape
    return pl.pallas_call(
        spread_kernel,
        out_shape=jax.ShapeDtypeStruct((devices, owned + 8, width), jnp.float32),
        in_specs=[pl.BlockSpec(memory_space=pltpu.SMEM), vmem],
        out_specs=vmem,
        name="spread_modes",
    )(targets, modes)


def modal_kernel(targets, reduced, modes, local_out):
    members, kinds, columns_total, _ = reduced.shape
    edges = targets.shape[1]
    parts = modes.shape[0] // PB
    owned = columns_total // edges // parts
    totals = [None] * kinds
    for c in range(members):
        picked = jnp.concatenate(
            [
                modes[targets[c, a] * parts + part, :owned, :]
                for a in range(edges)
                for part in range(parts)
            ],
            0,
        )
        turned = picked.T
        for kind in range(kinds):
            share = mm_high(turned, mm_high(reduced[c, kind], picked))
            totals[kind] = share if totals[kind] is None else totals[kind] + share
    for kind in range(kinds):
        local_out[kind] = totals[kind]


def modal_share(targets, reduced, modes):
    vmem = pl.BlockSpec(memory_space=pltpu.VMEM)
    width = modes.shape[2]
    return pl.pallas_call(
        modal_kernel,
        out_shape=jax.ShapeDtypeStruct((reduced.shape[1], width, width), jnp.float32),
        in_specs=[pl.BlockSpec(memory_space=pltpu.SMEM), vmem, vmem],
        out_specs=vmem,
        cost_estimate=pl.CostEstimate(
            flops=1_000_000_000, bytes_accessed=2_000_000, transcendentals=0
        ),
        name="modal_share",
    )(targets, reduced, modes)


def gather_kernel(stride, targets, bit, *refs):
    parts = len(refs) - 4
    pieces = refs[:parts]
    keep_out, send_out, total = refs[parts + 1 :]
    slots = total.shape[0]
    members, kinds, edges, _, columns_total = pieces[0].shape
    width = columns_total // edges
    total[...] = jnp.zeros_like(total)
    for m in range(parts):
        for c in range(members):
            where = [targets[(m * members + c) * edges + a] for a in range(edges)]
            for kind in range(kinds):
                for a in range(edges):
                    for b in range(edges):
                        at = pl.ds(pl.multiple_of(where[b] * width, width), width)
                        total[where[a], kind, :, at] += pieces[m][
                            c, kind, a, :, b * width : (b + 1) * width
                        ]
    mine = bit[0]
    for slot in range(slots // 2):
        first = (slot // stride) * 2 * stride + slot % stride
        keep_out[slot] = total[first + mine * stride]
        send_out[slot] = total[first + (1 - mine) * stride]


def gather_rows(targets, bit, stride, pieces, slots, after):
    _, kinds, edges, owned, columns_total = pieces[0].shape
    full = slots * (columns_total // edges)
    vmem = pl.BlockSpec(memory_space=pltpu.VMEM)
    smem = pl.BlockSpec(memory_space=pltpu.SMEM)
    half = jax.ShapeDtypeStruct((slots // 2, kinds, owned, full), jnp.float32)
    return pl.pallas_call(
        functools.partial(gather_kernel, stride),
        out_shape=(half, half),
        in_specs=[smem, smem] + [vmem] * len(pieces) + [pl.BlockSpec(memory_space=pl.ANY)],
        out_specs=(vmem, vmem),
        scratch_shapes=[pltpu.VMEM((slots, kinds, owned, full), jnp.float32)],
        cost_estimate=pl.CostEstimate(
            flops=100_000_000, bytes_accessed=4_000_000, transcendentals=0
        ),
        name="gather_rows",
    )(targets, bit, *pieces, after)


def on_device(
    interior_stiffness,
    interior_links,
    coupling_stiffness,
    interface_stiffness,
    interior_mass,
    interface_mass,
    interior_modes,
    interior_blocks,
    interface_blocks,
    parent_modes,
):
    cores = lax.axis_size("dev")
    devices = lax.axis_size("grp") * cores
    members, edges = interface_blocks.shape
    per_block = devices // PB
    me = lax.axis_index(AXES)

    def across(value, mask):
        return lax.ppermute(value, AXES, [(d, d ^ mask) for d in range(devices)])

    all_modes = lax.all_to_all(
        spread_modes(interface_blocks, parent_modes, devices),
        AXES, 0, 0, tiled=True,
    )
    reduced, coupling, *pieces = reduce_members(
        interior_blocks,
        (me % per_block)[None],
        per_block,
        interior_stiffness,
        interior_links,
        coupling_stiffness,
        interface_stiffness,
        interior_mass,
        interface_mass,
        interior_modes,
    )
    arrived = [pieces[0]] + [across(pieces[m], m) for m in range(1, per_block)]
    names = all_modes[:, parent_modes.shape[0], : members * edges].reshape(
        PB, per_block, members * edges
    )
    near = [
        lax.dynamic_slice(
            names, (me // per_block, (me % per_block) ^ m, 0), (1, 1, members * edges)
        ).reshape(-1)
        for m in range(per_block)
    ]
    targets = jnp.concatenate(near).astype(jnp.int32)
    scaling = (PB / (members * devices * edges)) ** 0.5
    core = (me // cores) % 2
    sides = [[d for d in range(devices) if (d // cores) % 2 == side] for side in range(2)]
    share = modal_share(interface_blocks, reduced, all_modes)
    ours = lax.dynamic_index_in_dim(share, core, 0, False)
    theirs = lax.dynamic_index_in_dim(share, 1 - core, 0, False)
    theirs = across(theirs, cores)
    ours = ours + theirs
    modes_total = ours.shape[1]
    modal_in = lax.all_to_all(
        ours.reshape(devices // 2, 2 * modes_total // devices, modes_total),
        AXES, 0, 0, tiled=True, axis_index_groups=sides,
    )
    modal_rows = modal_in.sum(0) * scaling
    modal_all = lax.all_to_all(
        jnp.broadcast_to(modal_rows[None], (devices // 2,) + modal_rows.shape),
        AXES, 0, 0, tiled=True, axis_index_groups=sides,
    ).reshape(modes_total, modes_total)
    modal_other = across(modal_all, cores)
    modal_stiffness = jnp.where(core == 0, modal_all, modal_other)
    modal_mass = jnp.where(core == 0, modal_other, modal_all)

    strides = [per_block << k for k in range(PB.bit_length() - 1)]
    first = cores
    remaining = sorted(strides, reverse=True)
    remaining.remove(first)
    bits = {stride: (me // stride) % 2 for stride in strides}
    keep, send = gather_rows(
        targets, bits[first][None], first // per_block, arrived, PB, share
    )
    tail = keep.shape[1:]
    got = across(send, first)
    shape = (2,) * len(remaining) + tail
    keep, got = keep.reshape(shape), got.reshape(shape)
    results = []
    for kind in range(tail[0]):
        pair = [lax.index_in_dim(value, kind, len(remaining), False) for value in (keep, got)]
        left = list(remaining)
        order = remaining if kind % 2 == 0 else remaining[::-1]
        for stride in order:
            axis = left.index(stride)
            left.remove(stride)

            def pick(which):
                return sum(lax.dynamic_index_in_dim(value, which, axis, False) for value in pair)

            received = across(pick(1 - bits[stride]), stride)
            pair = [pick(bits[stride]), received]
        results.append(sum(pair) * scaling)
    return (results[0], results[1], coupling, modal_stiffness, modal_mass)


def solution(mesh):
    placed = (
        P(AXES, None, None, None),
        P(AXES, None, None, None),
        P(AXES, None, None),
        P(AXES, None, None),
        P(AXES, None),
        P(AXES, None),
        P(AXES, None, None),
        P(AXES),
        P(AXES, None),
        P(AXES, None),
    )

    return jax.shard_map(
        on_device,
        mesh=mesh,
        in_specs=placed,
        out_specs=(P(AXES, None), P(AXES, None), P(AXES, None, None), P(), P()),
        check_vma=False,
    )
```

time: 145 us -> 122 us (0.84)
  waiting for transfers between devices: 42.9 us -> 29.4 us
  Pallas kernels: 50.5 us -> 38.3 us
  other arithmetic: 1.69 us -> 3.71 us
  starting transfers between devices: 38.8 us -> 40.3 us
    ppermute x9 -> x10, waiting for transfers between devices: 29.5 us -> 14 us  [across(): return lax.ppermute(value, AXES, [(d, d ^ mask) for d in range(devices)])]
    pallas_call x1, Pallas kernels: 42.3 us -> 29.6 us  [reduce_members(): pl.pallas_call(reduce_kernel, out_shape=(jax.ShapeDtypeStruct((members, 2...]
    unnamed x14 -> x28, local copies, waits for them, and re-layouts: 1.84 us -> 4.62 us
    slice x0 -> x3, local copies, waits for them, and re-layouts: none -> 2.28 us  [the longest x2 1.36 us: on_device(): lax.index_in_dim(value, kind, len(remaining), False)]
    all_to_all x3, starting transfers between devices: 19.4 us -> 21.6 us  [the longest x1 10.7 us: on_device(): lax.all_to_all(ours.reshape(devices // 2, 2 * modes_total // devices, mod...]
    pallas_call x0 -> x1, Pallas kernels: none -> 2.02 us  [spread_modes(): pl.pallas_call(spread_kernel, out_shape=jax.ShapeDtypeStruct((devices, ow...]
    broadcast_in_dim x2 -> x1, local copies, waits for them, and re-layouts: 2.72 us -> 0.73 us  [on_device(): jnp.broadcast_to(modal_rows[None], (devices // 2,) + modal_rows.shape)]
    all_to_all x3, waiting for transfers between devices: 13.4 us -> 15.4 us  [the longest x1 9.21 us: on_device(): lax.all_to_all(ours.reshape(devices // 2, 2 * modes_total // devices, mod...]
  transfers between devices with their start and end apart: 12 -> 13, of which waited for: 5 -> 6; matrix products, arithmetic and copies ran while one was open for 4% -> 6% of each run, Pallas kernels for 35% -> 30%
where the time goes in v2:
time: 122 us; the launch traced here: 121 us
  starting transfers between devices  40.3 us (33%)
  Pallas kernels  38.3 us (31%)
  waiting for transfers between devices  29.4 us (24%)
  local copies, waits for them, and re-layouts  8.68 us (7%)
  other arithmetic  3.71 us (3%)
    pallas_call x1, Pallas kernels, reduce_members(): pl.pallas_call(reduce_kernel, out_shape=(jax.ShapeDtypeStruct((members, 2...  29.6 us
    ppermute x10, starting transfers between devices, across(): return lax.ppermute(value, AXES, [(d, d ^ mask) for d in range(devices)])  18.7 us
    ppermute x10, waiting for transfers between devices, across(): return lax.ppermute(value, AXES, [(d, d ^ mask) for d in range(devices)])  14 us
    all_to_all x1, starting transfers between devices, on_device(): lax.all_to_all(ours.reshape(devices // 2, 2 * modes_total // devices, mod...  10.7 us
    all_to_all x1, waiting for transfers between devices, on_device(): lax.all_to_all(ours.reshape(devices // 2, 2 * modes_total // devices, mod...  9.21 us
    all_to_all x1, starting transfers between devices, on_device(): lax.all_to_all(spread_modes(interface_blocks, parent_modes, devices), AXE...  7.45 us
    all_to_all x1, waiting for transfers between devices, on_device(): lax.all_to_all(jnp.broadcast_to(modal_rows[None], (devices // 2,) + modal...  6.19 us
    unnamed x28, local copies, waits for them, and re-layouts  4.62 us
  transfers between devices with their start and end apart: 13, of which 6 were waited for; matrix products, arithmetic and copies ran while one was open for 6% of the time, Pallas kernels for 30%

profile of v2, /device:TPU:0, one launch (start us, length us, event | category | flops | bytes accessed | tf_op | source)
XLA Modules:
  0.0 121.2 jit_solution(4646650220718525860)
XLA Ops:
  0.6 0.0 copy-start.2
  0.6 2.0 %spread_modes.1 = f32[32,40,256]{2,1,0:T(8,128)} custom-call(s32[2,2]{1,0:T(2,128)} %targets.3, f32[32,256]{1,0:T(8,128)} %modes.2), custom_call_target="tpu_custom_call" | custom-call | tf_op jit(solution)/shard_map/spread_modes/pallas_call | solution.py:303
  2.7 0.0 copy-start.1
  2.7 0.0 copy-start.5
  2.7 0.0 copy-start.6
  2.7 0.0 copy-start.7
  2.7 0.0 copy-start.8
  2.7 7.4 %all-to-all-start = ((f32[32,40,256]{2,1,0:T(8,128)}), f32[32,40,256]{2,1,0:T(8,128)}, u32[]{:S(2)}, u32[]{:S(2)}) async-start(f32[32,40,256]{2,1,0:T(8,128)} %spread_modes.1), calls=%async_computation | async-start | bytes 2621440 | tf_op jit(solution)/shard_map/all_to_all | solution.py:415
  10.2 0.0 copy-done.2
  10.2 0.0 copy-done.1
  10.2 0.0 copy-done.5
  10.2 0.0 copy-done.6
  10.2 0.0 copy-done.7
  10.2 0.0 copy-done.8
  10.2 0.0 copy-start.3
  10.2 1.2 copy-done.3
  11.4 1.0 copy-done.4
  12.4 29.6 %reduce_members.1 = (f32[2,2,256,256]{3,2,1,0:T(8,128)S(1)}, f32[2,256,256]{2,1,0:T(8,128)}, f32[2,2,2,32,256]{4,3,2,1,0:T(8,128)S(1)}, f32[2,2,2,32,256]{4,3,2,...) custom-call(s32[2]{0:T(128)S(1)} %copy-done.8, s32[1]{0:T(128)} %bitcast.2.place, ...), custom_call_target="tpu_custom_call" | custom-call | flops 20000000000 | bytes 8000000 | tf_op jit(solution)/shard_map/reduce_members/pallas_call | solution.py:262
  42.0 0.7 copy-done
  42.7 1.0 copy-done.9
  43.7 8.6 %collective-permute-start = (f32[2,2,2,32,256]{4,3,2,1,0:T(8,128)}, f32[2,2,2,32,256]{4,3,2,1,0:T(8,128)S(1)}, u32[]{:S(2)}, u32[]{:S(2)}) collective-permute-start(f32[2,2,2,32,256]{4,3,2,1,0:T(8,128)} %get-tuple-element.14), channel_id=1, source_target_pairs={{0,1},{1,0},{2,3},{3,2},{4,5},{5,4},{6,7},{7,6},{8,9},{9,8},{10,11... | collective-permute-start | bytes 786440 | tf_op jit(solution)/shard_map/ppermute | solution.py:413
  52.3 0.0 collective-permute-start.1
  52.3 1.5 %collective-permute-start.2 = (f32[2,2,2,32,256]{4,3,2,1,0:T(8,128)}, f32[2,2,2,32,256]{4,3,2,1,0:T(8,128)S(1)}, u32[]{:S(2)}, u32[]{:S(2)}) collective-permute-start(f32[2,2,2,32,256]{4,3,2,1,0:T(8,128)} %get-tuple-element.16), channel_id=1, source_target_pairs={{0,3},{1,2},{2,1},{3,0},{4,7},{5,6},{6,5},{7,4},{8,11},{9,10},{10,... | collective-permute-start | bytes 786440 | tf_op jit(solution)/shard_map/ppermute | solution.py:413
  53.7 0.0 all-to-all-done.modes
  53.7 3.6 %modal_share.1.refs_4_ = f32[2,256,256]{2,1,0:T(8,128)} custom-call(s32[2,2]{1,0:T(2,128)} %targets.3, f32[2,2,256,256]{3,2,1,0:T(8,128)} %copy-done.9, f32[32,40,256]{2,1,0:T(8,128)} %all-to-all-done.modes), custom_call_target="tpu_custom_call" | custom-call | flops 1000000000 | bytes 2000000 | tf_op jit(solution)/shard_map/modal_share/pallas_call | solution.py:338
  57.3 1.0 dynamic-slice_bitcast_fusion
  58.4 0.1 collective-permute-start.8
  58.4 0.9 slice.20
  59.4 0.6 maximum_convert_fusion.targets
  60.0 0.0 collective-permute-done.refs_1_
  60.0 0.0 collective-permute-done.1.refs_2_
  60.0 0.0 copy-start.12
  60.0 1.1 collective-permute-done.2.refs_3_
  61.1 0.0 copy-done.11
  61.1 0.0 copy-done.12
  61.1 0.7 copy-done.13
  61.8 3.1 %gather_rows.1 = (f32[4,2,32,1024]{3,2,1,0:T(8,128)}, f32[4,2,32,1024]{3,2,1,0:T(8,128)}) custom-call(s32[16]{0:T(128)} %maximum_convert_fusion.targets, s32[1]{0:T(128)} %bitcast.1.bit, f32[2,2,2,32,256]{4,3,2,1,0:T(8,128)} %copy-done, f32[2,2,2,32,256]{4,3,2,1,0:T(8,128)} %copy-done.11, f32[2,2,2,32,256]{4,3,2,1,0:T(8,128)} %copy-done.12, ...), custom_call_target="tpu_custom_call" | custom-call | flops 100000000 | bytes 4000000 | tf_op jit(solution)/shard_map/gather_rows/pallas_call | solution.py:381
  64.9 0.0 collective-permute-start.3
  64.9 0.0 collective-permute-done.8
  64.9 0.0 copy-done.10
  64.9 0.7 bitcast_add_fusion.4
  65.6 10.7 %all-to-all-start.1 = ((f32[16,16,256]{2,1,0:T(8,128)}), f32[16,16,256]{2,1,0:T(8,128)S(1)}, u32[]{:S(2)}, u32[]{:S(2)}) async-start(f32[16,16,256]{2,1,0:T(8,128)} %bitcast.17), calls=%async_computation.1 | async-start | bytes 524288 | tf_op jit(solution)/shard_map/all_to_all | solution.py:451
  76.3 1.3 %fusion.10 = (f32[2,2,1,32,1024]{4,3,2,1,0:T(8,128)S(1)}, f32[2,2,1,32,1024]{4,3,2,1,0:T(8,128)S(1)}) fusion(f32[2,2,2,32,1024]{4,3,2,1,0:T(8,128)} %bitcast.76), kind=kLoop, calls=%fused_computation.30 | loop fusion | bytes 2097152 | tf_op jit(solution)/shard_map/slice | solution.py:478
  77.6 9.2 %all-to-all-done.1 = f32[16,16,256]{2,1,0:T(8,128)S(1)} async-done(((f32[16,16,256]{2,1,0:T(8,128)}), f32[16,16,256]{2,1,0:T(8,128)S(1)}, u32[]{:S(2)}, u32[]{:S(2)}) %all-to-all-start.1) | async-done | bytes 262176 | tf_op jit(solution)/shard_map/all_to_all | solution.py:451
  86.9 0.7 broadcast_in_dim.14
  87.6 3.5 %all-to-all-start.2 = ((f32[16,16,256]{2,1,0:T(8,128)}), f32[16,16,256]{2,1,0:T(8,128)S(1)}, u32[]{:S(2)}, u32[]{:S(2)}) async-start(f32[16,16,256]{2,1,0:T(8,128)} %broadcast_in_dim.14), calls=%async_computation.2 | async-start | bytes 524288 | tf_op jit(solution)/shard_map/all_to_all | solution.py:456
  91.1 0.0 collective-permute-done.3
  91.1 0.1 fusion.11
  91.2 0.1 bitcast_add_fusion.3
  91.3 1.9 %collective-permute-start.4 = (f32[2,32,1024]{2,1,0:T(8,128)S(1)}, f32[2,32,1024]{2,1,0:T(8,128)S(1)}, u32[]{:S(2)}, u32[]{:S(2)}) collective-permute-start(f32[2,32,1024]{2,1,0:T(8,128)S(1)} %get-tuple-element.28), channel_id=1, source_target_pairs={{0,16},{1,17},{2,18},{3,19},{4,20},{5,21},{6,22},{7,23},{8,24},{9,... | collective-permute-start | bytes 786440 | tf_op jit(solution)/shard_map/ppermute | solution.py:413
  93.2 0.1 bitcast_add_fusion.1
  93.3 2.5 %collective-permute-start.6 = (f32[2,32,1024]{2,1,0:T(8,128)S(1)}, f32[2,32,1024]{2,1,0:T(8,128)S(1)}, u32[]{:S(2)}, u32[]{:S(2)}) collective-permute-start(f32[2,32,1024]{2,1,0:T(8,128)S(1)} %get-tuple-element.22), channel_id=1, source_target_pairs={{0,4},{1,5},{2,6},{3,7},{4,0},{5,1},{6,2},{7,3},{8,12},{9,13},{10,... | collective-permute-start | bytes 786440 | tf_op jit(solution)/shard_map/ppermute | solution.py:413
  95.8 5.2 %collective-permute-done.4 = f32[2,32,1024]{2,1,0:T(8,128)S(1)} collective-permute-done((f32[2,32,1024]{2,1,0:T(8,128)S(1)}, f32[2,32,1024]{2,1,0:T(8,128)S(1)}, u32[]{:S(2)}, u32[]{:S(2)}) %collective-permute-start.4) | collective-permute-done | bytes 262176 | tf_op jit(solution)/shard_map/ppermute | solution.py:413
  101.0 2.7 %collective-permute-start.5 = (f32[32,1024]{1,0:T(8,128)S(1)}, f32[32,1024]{1,0:T(8,128)S(1)}, u32[]{:S(2)}, u32[]{:S(2)}) collective-permute-start(f32[32,1024]{1,0:T(8,128)S(1)} %fusion.4), channel_id=1, source_target_pairs={{0,4},{1,5},{2,6},{3,7},{4,0},{5,1},{6,2},{7,3},{8,12},{9,13},{10,... | collective-permute-start | bytes 393224 | tf_op jit(solution)/shard_map/ppermute | solution.py:413
  103.6 6.2 %all-to-all-done.2 = f32[16,16,256]{2,1,0:T(8,128)S(1)} async-done(((f32[16,16,256]{2,1,0:T(8,128)}), f32[16,16,256]{2,1,0:T(8,128)S(1)}, u32[]{:S(2)}, u32[]{:S(2)}) %all-to-all-start.2) | async-done | bytes 262176 | tf_op jit(solution)/shard_map/all_to_all | solution.py:456
  109.8 0.0 collective-permute-start.9
  109.8 4.9 %collective-permute-done.6 = f32[2,32,1024]{2,1,0:T(8,128)S(1)} collective-permute-done((f32[2,32,1024]{2,1,0:T(8,128)S(1)}, f32[2,32,1024]{2,1,0:T(8,128)S(1)}, u32[]{:S(2)}, u32[]{:S(2)}) %collective-permute-start.6) | collective-permute-done | bytes 262176 | tf_op jit(solution)/shard_map/ppermute | solution.py:413
  114.7 1.5 %collective-permute-start.7 = (f32[32,1024]{1,0:T(8,128)S(1)}, f32[32,1024]{1,0:T(8,128)S(1)}, u32[]{:S(2)}, u32[]{:S(2)}) collective-permute-start(f32[32,1024]{1,0:T(8,128)S(1)} %fusion.2), channel_id=1, source_target_pairs={{0,16},{1,17},{2,18},{3,19},{4,20},{5,21},{6,22},{7,23},{8,24},{9,... | collective-permute-start | bytes 393224 | tf_op jit(solution)/shard_map/ppermute | solution.py:413
  116.2 0.0 collective-permute-done.5
  116.2 0.7 fusion.5
  116.9 2.8 %collective-permute-done.7 = f32[32,1024]{1,0:T(8,128)S(1)} collective-permute-done((f32[32,1024]{1,0:T(8,128)S(1)}, f32[32,1024]{1,0:T(8,128)S(1)}, u32[]{:S(2)}, u32[]{:S(2)}) %collective-permute-start.7) | collective-permute-done | bytes 131104 | tf_op jit(solution)/shard_map/ppermute | solution.py:413
  119.7 0.7 fusion.3
  120.4 0.0 collective-permute-done.9
  120.4 0.8 broadcast_select_fusion
  (11 shorter events, 0.1 us)
Async XLA Ops:
  0.6 9.5 %copy-start.2 = (f32[2,8,128,128]{3,2,1,0:T(8,128)S(1)}, f32[2,8,128,128]{3,2,1,0:T(8,128)}, u32[]{:S(2)}) copy-start(f32[2,8,128,128]{3,2,1,0:T(8,128)} %diag.1) | copy-start | bytes 3145732
  2.7 7.5 %copy-start.1 = (f32[2,1024,256]{2,1,0:T(8,128)S(1)}, f32[2,1024,256]{2,1,0:T(8,128)}, u32[]{:S(2)}) copy-start(f32[2,1024,256]{2,1,0:T(8,128)} %modes.3) | copy-start | bytes 6291460
  2.7 7.5 %copy-start.5 = (f32[2,128,256]{2,1,0:T(8,128)S(1)}, f32[2,128,256]{2,1,0:T(8,128)}, u32[]{:S(2)}) copy-start(f32[2,128,256]{2,1,0:T(8,128)} %coupled.1) | copy-start | bytes 786436
  2.7 7.5 %copy-start.6 = (f32[2,1024]{1,0:T(2,128)S(1)}, f32[2,1024]{1,0:T(2,128)}, u32[]{:S(2)}) copy-start(f32[2,1024]{1,0:T(2,128)} %inner_mass.1) | copy-start | bytes 24580
  2.7 7.5 %copy-start.7 = (f32[2,256]{1,0:T(2,128)S(1)}, f32[2,256]{1,0:T(2,128)}, u32[]{:S(2)}) copy-start(f32[2,256]{1,0:T(2,128)} %edge_mass.1) | copy-start | bytes 6148
  2.7 7.5 %copy-start.8 = (s32[2]{0:T(128)S(1)}, s32[2]{0:T(128)}, u32[]{:S(2)}) copy-start(s32[2]{0:T(128)} %counts.1) | copy-start | bytes 28
  2.7 51.0 %all-to-all-start = ((f32[32,40,256]{2,1,0:T(8,128)}), f32[32,40,256]{2,1,0:T(8,128)}, u32[]{:S(2)}, u32[]{:S(2)}) async-start(f32[32,40,256]{2,1,0:T(8,128)} %spread_modes.1), calls=%async_computation | async-start | bytes 2621440 | tf_op jit(solution)/shard_map/all_to_all | solution.py:415
  10.2 1.2 copy-start.3
  11.4 1.0 copy-start.4
  42.0 0.7 copy-start
  42.7 1.0 copy-start.9
  43.7 16.3 %collective-permute-start = (f32[2,2,2,32,256]{4,3,2,1,0:T(8,128)}, f32[2,2,2,32,256]{4,3,2,1,0:T(8,128)S(1)}, u32[]{:S(2)}, u32[]{:S(2)}) collective-permute-start(f32[2,2,2,32,256]{4,3,2,1,0:T(8,128)} %get-tuple-element.14), channel_id=1, source_target_pairs={{0,1},{1,0},{2,3},{3,2},{4,5},{5,4},{6,7},{7,6},{8,9},{9,8},{10,11... | collective-permute-start | bytes 786440 | tf_op jit(solution)/shard_map/ppermute | solution.py:413
  52.3 7.7 %collective-permute-start.1 = (f32[2,2,2,32,256]{4,3,2,1,0:T(8,128)}, f32[2,2,2,32,256]{4,3,2,1,0:T(8,128)S(1)}, u32[]{:S(2)}, u32[]{:S(2)}) collective-permute-start(f32[2,2,2,32,256]{4,3,2,1,0:T(8,128)} %get-tuple-element.15), channel_id=1, source_target_pairs={{0,2},{1,3},{2,0},{3,1},{4,6},{5,7},{6,4},{7,5},{8,10},{9,11},{10,... | collective-permute-start | bytes 786440 | tf_op jit(solution)/shard_map/ppermute | solution.py:413
  52.3 8.8 %collective-permute-start.2 = (f32[2,2,2,32,256]{4,3,2,1,0:T(8,128)}, f32[2,2,2,32,256]{4,3,2,1,0:T(8,128)S(1)}, u32[]{:S(2)}, u32[]{:S(2)}) collective-permute-start(f32[2,2,2,32,256]{4,3,2,1,0:T(8,128)} %get-tuple-element.16), channel_id=1, source_target_pairs={{0,3},{1,2},{2,1},{3,0},{4,7},{5,6},{6,5},{7,4},{8,11},{9,10},{10,... | collective-permute-start | bytes 786440 | tf_op jit(solution)/shard_map/ppermute | solution.py:413
  57.3 7.6 %copy-start.10 = (f32[2,256,256]{2,1,0:T(8,128)S(1)}, f32[2,256,256]{2,1,0:T(8,128)}, u32[]{:S(2)}) copy-start(f32[2,256,256]{2,1,0:T(8,128)} %modal_share.1.refs_4_) | copy-start | bytes 1572868
  58.4 6.5 %collective-permute-start.8 = (f32[256,256]{1,0:T(8,128)S(1)}, f32[256,256]{1,0:T(8,128)S(1)}, u32[]{:S(2)}, u32[]{:S(2)}) collective-permute-start(f32[256,256]{1,0:T(8,128)S(1)} %dynamic-slice_bitcast_fusion), channel_id=1, source_target_pairs={{0,8},{1,9},{2,10},{3,11},{4,12},{5,13},{6,14},{7,15},{8,0},{9,1},... | collective-permute-start | bytes 786440 | tf_op jit(solution)/shard_map/ppermute | solution.py:413
  60.0 1.1 copy-start.11
  60.0 1.1 copy-start.12
  61.1 0.7 copy-start.13
  64.9 26.3 %collective-permute-start.3 = (f32[4,2,32,1024]{3,2,1,0:T(8,128)}, f32[4,2,32,1024]{3,2,1,0:T(8,128)S(1)}, u32[]{:S(2)}, u32[]{:S(2)}) collective-permute-start(f32[4,2,32,1024]{3,2,1,0:T(8,128)} %get-tuple-element.19), channel_id=1, source_target_pairs={{0,8},{1,9},{2,10},{3,11},{4,12},{5,13},{6,14},{7,15},{8,0},{9,1},... | collective-permute-start | bytes 3145736 | tf_op jit(solution)/shard_map/ppermute | solution.py:413
  65.6 21.2 %all-to-all-start.1 = ((f32[16,16,256]{2,1,0:T(8,128)}), f32[16,16,256]{2,1,0:T(8,128)S(1)}, u32[]{:S(2)}, u32[]{:S(2)}) async-start(f32[16,16,256]{2,1,0:T(8,128)} %bitcast.17), calls=%async_computation.1 | async-start | bytes 524288 | tf_op jit(solution)/shard_map/all_to_all | solution.py:451
  87.6 22.2 %all-to-all-start.2 = ((f32[16,16,256]{2,1,0:T(8,128)}), f32[16,16,256]{2,1,0:T(8,128)S(1)}, u32[]{:S(2)}, u32[]{:S(2)}) async-start(f32[16,16,256]{2,1,0:T(8,128)} %broadcast_in_dim.14), calls=%async_computation.2 | async-start | bytes 524288 | tf_op jit(solution)/shard_map/all_to_all | solution.py:456
  91.3 9.6 %collective-permute-start.4 = (f32[2,32,1024]{2,1,0:T(8,128)S(1)}, f32[2,32,1024]{2,1,0:T(8,128)S(1)}, u32[]{:S(2)}, u32[]{:S(2)}) collective-permute-start(f32[2,32,1024]{2,1,0:T(8,128)S(1)} %get-tuple-element.28), channel_id=1, source_target_pairs={{0,16},{1,17},{2,18},{3,19},{4,20},{5,21},{6,22},{7,23},{8,24},{9,... | collective-permute-start | bytes 786440 | tf_op jit(solution)/shard_map/ppermute | solution.py:413
  93.3 21.4 %collective-permute-start.6 = (f32[2,32,1024]{2,1,0:T(8,128)S(1)}, f32[2,32,1024]{2,1,0:T(8,128)S(1)}, u32[]{:S(2)}, u32[]{:S(2)}) collective-permute-start(f32[2,32,1024]{2,1,0:T(8,128)S(1)} %get-tuple-element.22), channel_id=1, source_target_pairs={{0,4},{1,5},{2,6},{3,7},{4,0},{5,1},{6,2},{7,3},{8,12},{9,13},{10,... | collective-permute-start | bytes 786440 | tf_op jit(solution)/shard_map/ppermute | solution.py:413
  101.0 15.3 %collective-permute-start.5 = (f32[32,1024]{1,0:T(8,128)S(1)}, f32[32,1024]{1,0:T(8,128)S(1)}, u32[]{:S(2)}, u32[]{:S(2)}) collective-permute-start(f32[32,1024]{1,0:T(8,128)S(1)} %fusion.4), channel_id=1, source_target_pairs={{0,4},{1,5},{2,6},{3,7},{4,0},{5,1},{6,2},{7,3},{8,12},{9,13},{10,... | collective-permute-start | bytes 393224 | tf_op jit(solution)/shard_map/ppermute | solution.py:413
  109.8 10.6 %collective-permute-start.9 = (f32[256,256]{1,0:T(8,128)S(1)}, f32[256,256]{1,0:T(8,128)S(1)}, u32[]{:S(2)}, u32[]{:S(2)}) collective-permute-start(f32[256,256]{1,0:T(8,128)S(1)} %bitcast.77), channel_id=1, source_target_pairs={{0,8},{1,9},{2,10},{3,11},{4,12},{5,13},{6,14},{7,15},{8,0},{9,1},... | collective-permute-start | bytes 786440 | tf_op jit(solution)/shard_map/ppermute | solution.py:413
  114.7 5.0 %collective-permute-start.7 = (f32[32,1024]{1,0:T(8,128)S(1)}, f32[32,1024]{1,0:T(8,128)S(1)}, u32[]{:S(2)}, u32[]{:S(2)}) collective-permute-start(f32[32,1024]{1,0:T(8,128)S(1)} %fusion.2), channel_id=1, source_target_pairs={{0,16},{1,17},{2,18},{3,19},{4,20},{5,21},{6,22},{7,23},{8,24},{9,... | collective-permute-start | bytes 393224 | tf_op jit(solution)/shard_map/ppermute | solution.py:413

commit v3 on v2

--- a/solution.py
+++ b/solution.py
@@ -148,8 +148,10 @@
     counts, place, diag, links, coupled, edge, inner_mass, edge_mass, modes,
     reduced_out, coupling_out, *rest,
 ):
-    pieces_out = rest[:-6]
-    work, state, moved, ahead, source, solved = rest[-6:]
+    pieces_out = rest[:-8]
+    work, state, moved, ahead, source, solved, modes_here, modes_semaphore = rest[-8:]
+    modes_copy = pltpu.make_async_copy(modes, modes_here, modes_semaphore)
+    modes_copy.start()
     members, blocks, width, _ = diag.shape
     chains = 2 * members
     columns_total = coupled.shape[2]
@@ -224,6 +226,7 @@
         return carry
 
     lax.fori_loop(0, levels, back, 0)
+    modes_copy.wait()
     row = lax.broadcasted_iota(jnp.int32, (columns_total, columns_total), 0)
     column = lax.broadcasted_iota(jnp.int32, (columns_total, columns_total), 1)
     for c in range(members):
@@ -234,7 +237,7 @@
         heavy = flat.T * weight
         diagonal = jnp.where(row == column, edge_mass[c : c + 1, :], 0.0)
         reduced_out[c, 1] = diagonal + mm_high(heavy, flat)
-        coupling_out[c] = mm_high(jnp.where(inside, modes[c].T, 0.0) * weight, flat)
+        coupling_out[c] = mm_high(jnp.where(inside, modes_here[c].T, 0.0) * weight, flat)
 
 
     parts = len(pieces_out)
@@ -266,7 +269,7 @@
             jax.ShapeDtypeStruct((members, modes_total, columns_total), f32),
         )
         + (piece,) * parts,
-        in_specs=[smem, smem] + [vmem] * 7,
+        in_specs=[smem, smem] + [vmem] * 6 + [pl.BlockSpec(memory_space=pl.ANY)],
         out_specs=(vmem,) * (2 + parts),
         scratch_shapes=[
             pltpu.VMEM((2 * members, width, width), f32),
@@ -275,11 +278,12 @@
             pltpu.VMEM((depth, members, width, columns_total), f32),
             pltpu.VMEM((members, width, columns_total), f32),
             pltpu.VMEM((members, blocks + 1, width, columns_total), f32),
+            pltpu.VMEM(modes.shape, f32),
+            pltpu.SemaphoreType.DMA(()),
         ],
         cost_estimate=pl.CostEstimate(
             flops=20_000_000_000, bytes_accessed=8_000_000, transcendentals=0
         ),
-        compiler_params=pltpu.CompilerParams(vmem_limit_bytes=24 * 1024 * 1024),
         name="reduce_members",
     )(counts, place, diag, links, coupled, edge, inner_mass, edge_mass, modes)
 
@@ -309,7 +313,7 @@
     )(targets, modes)
 
 
-def modal_kernel(targets, reduced, modes, local_out):
+def modal_kernel(targets, side, reduced, modes, ours_out, theirs_out, both):
     members, kinds, columns_total, _ = reduced.shape
     edges = targets.shape[1]
     parts = modes.shape[0] // PB
@@ -329,22 +333,26 @@
             share = mm_high(turned, mm_high(reduced[c, kind], picked))
             totals[kind] = share if totals[kind] is None else totals[kind] + share
     for kind in range(kinds):
-        local_out[kind] = totals[kind]
-
-
-def modal_share(targets, reduced, modes):
+        both[kind] = totals[kind]
+    ours_out[...] = both[side[0]]
+    theirs_out[...] = both[1 - side[0]]
+
+
+def modal_share(targets, side, reduced, modes):
     vmem = pl.BlockSpec(memory_space=pltpu.VMEM)
+    smem = pl.BlockSpec(memory_space=pltpu.SMEM)
     width = modes.shape[2]
     return pl.pallas_call(
         modal_kernel,
-        out_shape=jax.ShapeDtypeStruct((reduced.shape[1], width, width), jnp.float32),
-        in_specs=[pl.BlockSpec(memory_space=pltpu.SMEM), vmem, vmem],
-        out_specs=vmem,
+        out_shape=(jax.ShapeDtypeStruct((width, width), jnp.float32),) * 2,
+        in_specs=[smem, smem, vmem, vmem],
+        out_specs=(vmem, vmem),
+        scratch_shapes=[pltpu.VMEM((reduced.shape[1], width, width), jnp.float32)],
         cost_estimate=pl.CostEstimate(
             flops=1_000_000_000, bytes_accessed=2_000_000, transcendentals=0
         ),
         name="modal_share",
-    )(targets, reduced, modes)
+    )(targets, side, reduced, modes)
 
 
 def gather_kernel(stride, targets, bit, *refs):
@@ -442,14 +450,12 @@
     scaling = (PB / (members * devices * edges)) ** 0.5
     core = (me // cores) % 2
     sides = [[d for d in range(devices) if (d // cores) % 2 == side] for side in range(2)]
-    share = modal_share(interface_blocks, reduced, all_modes)
-    ours = lax.dynamic_index_in_dim(share, core, 0, False)
-    theirs = lax.dynamic_index_in_dim(share, 1 - core, 0, False)
+    ours, theirs = modal_share(interface_blocks, core[None], reduced, all_modes)
     theirs = across(theirs, cores)
-    ours = ours + theirs
-    modes_total = ours.shape[1]
+    summed = ours + theirs
+    modes_total = summed.shape[1]
     modal_in = lax.all_to_all(
-        ours.reshape(devices // 2, 2 * modes_total // devices, modes_total),
+        summed.reshape(devices // 2, 2 * modes_total // devices, modes_total),
         AXES, 0, 0, tiled=True, axis_index_groups=sides,
     )
     modal_rows = modal_in.sum(0) * scaling
@@ -467,7 +473,7 @@
     remaining.remove(first)
     bits = {stride: (me // stride) % 2 for stride in strides}
     keep, send = gather_rows(
-        targets, bits[first][None], first // per_block, arrived, PB, share
+        targets, bits[first][None], first // per_block, arrived, PB, ours
     )
     tail = keep.shape[1:]
     got = across(send, first)

time: 122 us -> 122 us (level)
  local copies, waits for them, and re-layouts: 8.68 us -> 4.88 us
  waiting for transfers between devices: 29.4 us -> 31.5 us
  Pallas kernels: 38.3 us -> 39.8 us
    unnamed x28 -> x12, local copies, waits for them, and re-layouts: 4.62 us -> 1.8 us
    ppermute x10, waiting for transfers between devices: 14 us -> 16.5 us  [across(): return lax.ppermute(value, AXES, [(d, d ^ mask) for d in range(devices)])]
    pallas_call x1, Pallas kernels: 29.6 us -> 31.2 us  [reduce_members(): pl.pallas_call(reduce_kernel, out_shape=(jax.ShapeDtypeStruct((members, 2...]
  transfers between devices with their start and end apart: 13 -> 13, of which waited for: 6 -> 7; matrix products, arithmetic and copies ran while one was open for 6% -> 5% of each run, Pallas kernels for 30% -> 29%
where the time goes in v3:
time: 122 us; the launch traced here: 121 us
  starting transfers between devices  40.8 us (33%)
  Pallas kernels  39.8 us (33%)
  waiting for transfers between devices  31.5 us (26%)
  local copies, waits for them, and re-layouts  4.88 us (4%)
  other arithmetic  3.71 us (3%)
    pallas_call x1, Pallas kernels, reduce_members(): pl.pallas_call(reduce_kernel, out_shape=(jax.ShapeDtypeStruct((members, 2...  31.2 us
    ppermute x10, starting transfers between devices, across(): return lax.ppermute(value, AXES, [(d, d ^ mask) for d in range(devices)])  19.4 us
    ppermute x10, waiting for transfers between devices, across(): return lax.ppermute(value, AXES, [(d, d ^ mask) for d in range(devices)])  16.5 us
    all_to_all x1, starting transfers between devices, on_device(): lax.all_to_all(summed.reshape(devices // 2, 2 * modes_total // devices, m...  10.6 us
    all_to_all x1, waiting for transfers between devices, on_device(): lax.all_to_all(summed.reshape(devices // 2, 2 * modes_total // devices, m...  8.85 us
    all_to_all x1, starting transfers between devices, on_device(): lax.all_to_all(spread_modes(interface_blocks, parent_modes, devices), AXE...  7.33 us
    all_to_all x1, waiting for transfers between devices, on_device(): lax.all_to_all(jnp.broadcast_to(modal_rows[None], (devices // 2,) + modal...  6.12 us
    pallas_call x1, Pallas kernels, modal_share(): pl.pallas_call(modal_kernel, out_shape=(jax.ShapeDtypeStruct((width, widt...  3.62 us
  transfers between devices with their start and end apart: 13, of which 7 were waited for; matrix products, arithmetic and copies ran while one was open for 5% of the time, Pallas kernels for 29%

profile of v3, /device:TPU:0, one launch (start us, length us, event | category | flops | bytes accessed | tf_op | source)
XLA Modules:
  0.0 121.5 jit_solution(12751644834527049106)
XLA Ops:
  0.6 1.9 %spread_modes.1 = f32[32,40,256]{2,1,0:T(8,128)} custom-call(s32[2,2]{1,0:T(2,128)} %targets.3, f32[32,256]{1,0:T(8,128)} %modes.2), custom_call_target="tpu_custom_call" | custom-call | tf_op jit(solution)/shard_map/spread_modes/pallas_call | solution.py:307
  2.6 7.3 %all-to-all-start = ((f32[32,40,256]{2,1,0:T(8,128)}), f32[32,40,256]{2,1,0:T(8,128)S(1)}, u32[]{:S(2)}, u32[]{:S(2)}) async-start(f32[32,40,256]{2,1,0:T(8,128)} %spread_modes.1), calls=%async_computation | async-start | bytes 2621440 | tf_op jit(solution)/shard_map/all_to_all | solution.py:423
  9.9 31.2 %reduce_members.1 = (f32[2,2,256,256]{3,2,1,0:T(8,128)}, f32[2,256,256]{2,1,0:T(8,128)}, f32[2,2,2,32,256]{4,3,2,1,0:T(8,128)}, f32[2,2,2,32,256]{4,3,2,1,0:T(8,...) custom-call(s32[2]{0:T(128)} %counts.1, s32[1]{0:T(128)} %bitcast.2.place, f32[2,8,128,128]{3,2,1,0:T(8,128)} %diag.1, ...), custom_call_target="tpu_custom_call" | custom-call | flops 20000000000 | bytes 8000000 | tf_op jit(solution)/shard_map/reduce_members/pallas_call | solution.py:265
  41.1 8.7 %collective-permute-start = (f32[2,2,2,32,256]{4,3,2,1,0:T(8,128)}, f32[2,2,2,32,256]{4,3,2,1,0:T(8,128)S(1)}, u32[]{:S(2)}, u32[]{:S(2)}) collective-permute-start(f32[2,2,2,32,256]{4,3,2,1,0:T(8,128)} %get-tuple-element.16), channel_id=1, source_target_pairs={{0,1},{1,0},{2,3},{3,2},{4,5},{5,4},{6,7},{7,6},{8,9},{9,8},{10,11... | collective-permute-start | bytes 786440 | tf_op jit(solution)/shard_map/ppermute | solution.py:421
  49.8 0.0 collective-permute-start.1
  49.8 1.5 %collective-permute-start.2 = (f32[2,2,2,32,256]{4,3,2,1,0:T(8,128)}, f32[2,2,2,32,256]{4,3,2,1,0:T(8,128)S(1)}, u32[]{:S(2)}, u32[]{:S(2)}) collective-permute-start(f32[2,2,2,32,256]{4,3,2,1,0:T(8,128)} %get-tuple-element.18), channel_id=1, source_target_pairs={{0,3},{1,2},{2,1},{3,0},{4,7},{5,6},{6,5},{7,4},{8,11},{9,10},{10,... | collective-permute-start | bytes 786440 | tf_op jit(solution)/shard_map/ppermute | solution.py:421
  51.3 0.0 all-to-all-done.modes
  51.3 0.0 copy-start
  51.3 1.1 copy-done
  52.4 3.6 %modal_share.1 = (f32[256,256]{1,0:T(8,128)}, f32[256,256]{1,0:T(8,128)}) custom-call(s32[2,2]{1,0:T(2,128)} %targets.3, s32[1]{0:T(128)} %bitcast.1.side.bit, f32[2,2,256,256]{3,2,1,0:T(8,128)} %get-tuple-element.19.reduced, f32[32,40,256]{2,1,0:T(8,128)} %copy-done), custom_call_target="tpu_custom_call" | custom-call | flops 1000000000 | bytes 2000000 | tf_op jit(solution)/shard_map/modal_share/pallas_call | solution.py:345
  56.0 0.0 copy-start.5
  56.0 0.0 copy-start.1
  56.0 1.0 slice.20
  57.0 0.6 maximum_convert_fusion.targets
  57.6 0.0 collective-permute-done.refs_1_
  57.6 0.0 copy-start.2
  57.6 0.0 collective-permute-done.1.refs_2_
  57.6 0.0 copy-start.3
  57.6 1.0 collective-permute-done.2.refs_3_
  58.7 0.0 copy-start.4
  58.7 0.0 copy-done.2
  58.7 0.0 copy-done.3
  58.7 0.7 copy-done.4
  59.4 3.1 %gather_rows.1 = (f32[4,2,32,1024]{3,2,1,0:T(8,128)}, f32[4,2,32,1024]{3,2,1,0:T(8,128)}) custom-call(s32[16]{0:T(128)} %maximum_convert_fusion.targets, s32[1]{0:T(128)} %bitcast.1.side.bit, f32[2,2,2,32,256]{4,3,2,1,0:T(8,128)} %get-tuple-element.15.refs_0_, f32[2,2,2,32,256]{4,3,2,1,0:T(8,128)} %copy-done.2, f32[2,2,2,32,256]{4,3,2,1,0:T(8,128)} %copy-done.3, ...), custom_call_target="tpu_custom_call" | custom-call | flops 100000000 | bytes 4000000 | tf_op jit(solution)/shard_map/gather_rows/pallas_call | solution.py:389
  62.5 0.0 collective-permute-start.3
  62.5 0.0 copy-done.5
  62.5 0.5 collective-permute-start.8
  63.0 2.7 %collective-permute-done.8 = f32[256,256]{1,0:T(8,128)S(1)} collective-permute-done((f32[256,256]{1,0:T(8,128)S(1)}, f32[256,256]{1,0:T(8,128)S(1)}, u32[]{:S(2)}, u32[]{:S(2)}) %collective-permute-start.8) | collective-permute-done | bytes 262176 | tf_op jit(solution)/shard_map/ppermute | solution.py:421
  65.7 0.0 copy-done.1
  65.7 0.7 add.154
  66.5 10.6 %all-to-all-start.1 = ((f32[16,16,256]{2,1,0:T(8,128)}), f32[16,16,256]{2,1,0:T(8,128)S(1)}, u32[]{:S(2)}, u32[]{:S(2)}) async-start(f32[16,16,256]{2,1,0:T(8,128)} %bitcast.15), calls=%async_computation.1 | async-start | bytes 524288 | tf_op jit(solution)/shard_map/all_to_all | solution.py:457
  77.1 1.3 %fusion.10 = (f32[2,2,1,32,1024]{4,3,2,1,0:T(8,128)S(1)}, f32[2,2,1,32,1024]{4,3,2,1,0:T(8,128)S(1)}) fusion(f32[2,2,2,32,1024]{4,3,2,1,0:T(8,128)} %bitcast.72), kind=kLoop, calls=%fused_computation.28 | loop fusion | bytes 2097152 | tf_op jit(solution)/shard_map/slice | solution.py:484
  78.4 8.9 %all-to-all-done.1 = f32[16,16,256]{2,1,0:T(8,128)S(1)} async-done(((f32[16,16,256]{2,1,0:T(8,128)}), f32[16,16,256]{2,1,0:T(8,128)S(1)}, u32[]{:S(2)}, u32[]{:S(2)}) %all-to-all-start.1) | async-done | bytes 262176 | tf_op jit(solution)/shard_map/all_to_all | solution.py:457
  87.3 0.7 broadcast_in_dim.15
  88.0 3.5 %all-to-all-start.2 = ((f32[16,16,256]{2,1,0:T(8,128)}), f32[16,16,256]{2,1,0:T(8,128)S(1)}, u32[]{:S(2)}, u32[]{:S(2)}) async-start(f32[16,16,256]{2,1,0:T(8,128)} %broadcast_in_dim.15), calls=%async_computation.2 | async-start | bytes 524288 | tf_op jit(solution)/shard_map/all_to_all | solution.py:462
  91.5 0.0 collective-permute-done.3
  91.6 0.1 fusion.11
  91.6 0.1 bitcast_add_fusion.3
  91.7 1.9 %collective-permute-start.4 = (f32[2,32,1024]{2,1,0:T(8,128)S(1)}, f32[2,32,1024]{2,1,0:T(8,128)S(1)}, u32[]{:S(2)}, u32[]{:S(2)}) collective-permute-start(f32[2,32,1024]{2,1,0:T(8,128)S(1)} %get-tuple-element.32), channel_id=1, source_target_pairs={{0,16},{1,17},{2,18},{3,19},{4,20},{5,21},{6,22},{7,23},{8,24},{9,... | collective-permute-start | bytes 786440 | tf_op jit(solution)/shard_map/ppermute | solution.py:421
  93.6 0.1 bitcast_add_fusion.1
  93.7 2.5 %collective-permute-start.6 = (f32[2,32,1024]{2,1,0:T(8,128)S(1)}, f32[2,32,1024]{2,1,0:T(8,128)S(1)}, u32[]{:S(2)}, u32[]{:S(2)}) collective-permute-start(f32[2,32,1024]{2,1,0:T(8,128)S(1)} %get-tuple-element.26), channel_id=1, source_target_pairs={{0,4},{1,5},{2,6},{3,7},{4,0},{5,1},{6,2},{7,3},{8,12},{9,13},{10,... | collective-permute-start | bytes 786440 | tf_op jit(solution)/shard_map/ppermute | solution.py:421
  96.2 5.0 %collective-permute-done.4 = f32[2,32,1024]{2,1,0:T(8,128)S(1)} collective-permute-done((f32[2,32,1024]{2,1,0:T(8,128)S(1)}, f32[2,32,1024]{2,1,0:T(8,128)S(1)}, u32[]{:S(2)}, u32[]{:S(2)}) %collective-permute-start.4) | collective-permute-done | bytes 262176 | tf_op jit(solution)/shard_map/ppermute | solution.py:421
  101.2 2.7 %collective-permute-start.5 = (f32[32,1024]{1,0:T(8,128)S(1)}, f32[32,1024]{1,0:T(8,128)S(1)}, u32[]{:S(2)}, u32[]{:S(2)}) collective-permute-start(f32[32,1024]{1,0:T(8,128)S(1)} %fusion.4), channel_id=1, source_target_pairs={{0,4},{1,5},{2,6},{3,7},{4,0},{5,1},{6,2},{7,3},{8,12},{9,13},{10,... | collective-permute-start | bytes 393224 | tf_op jit(solution)/shard_map/ppermute | solution.py:421
  103.9 6.1 %all-to-all-done.2 = f32[16,16,256]{2,1,0:T(8,128)S(1)} async-done(((f32[16,16,256]{2,1,0:T(8,128)}), f32[16,16,256]{2,1,0:T(8,128)S(1)}, u32[]{:S(2)}, u32[]{:S(2)}) %all-to-all-start.2) | async-done | bytes 262176 | tf_op jit(solution)/shard_map/all_to_all | solution.py:462
  110.0 0.0 collective-permute-start.9
  110.0 4.9 %collective-permute-done.6 = f32[2,32,1024]{2,1,0:T(8,128)S(1)} collective-permute-done((f32[2,32,1024]{2,1,0:T(8,128)S(1)}, f32[2,32,1024]{2,1,0:T(8,128)S(1)}, u32[]{:S(2)}, u32[]{:S(2)}) %collective-permute-start.6) | collective-permute-done | bytes 262176 | tf_op jit(solution)/shard_map/ppermute | solution.py:421
  114.9 1.5 %collective-permute-start.7 = (f32[32,1024]{1,0:T(8,128)S(1)}, f32[32,1024]{1,0:T(8,128)S(1)}, u32[]{:S(2)}, u32[]{:S(2)}) collective-permute-start(f32[32,1024]{1,0:T(8,128)S(1)} %fusion.2), channel_id=1, source_target_pairs={{0,16},{1,17},{2,18},{3,19},{4,20},{5,21},{6,22},{7,23},{8,24},{9,... | collective-permute-start | bytes 393224 | tf_op jit(solution)/shard_map/ppermute | solution.py:421
  116.5 0.0 collective-permute-done.5
  116.5 0.7 fusion.5
  117.1 2.8 %collective-permute-done.7 = f32[32,1024]{1,0:T(8,128)S(1)} collective-permute-done((f32[32,1024]{1,0:T(8,128)S(1)}, f32[32,1024]{1,0:T(8,128)S(1)}, u32[]{:S(2)}, u32[]{:S(2)}) %collective-permute-start.7) | collective-permute-done | bytes 131104 | tf_op jit(solution)/shard_map/ppermute | solution.py:421
  120.0 0.7 fusion.3
  120.6 0.0 collective-permute-done.9
  120.6 0.8 broadcast_select_fusion
  (5 shorter events, 0.1 us)
Async XLA Ops:
  2.6 48.8 %all-to-all-start = ((f32[32,40,256]{2,1,0:T(8,128)}), f32[32,40,256]{2,1,0:T(8,128)S(1)}, u32[]{:S(2)}, u32[]{:S(2)}) async-start(f32[32,40,256]{2,1,0:T(8,128)} %spread_modes.1), calls=%async_computation | async-start | bytes 2621440 | tf_op jit(solution)/shard_map/all_to_all | solution.py:423
  41.1 16.5 %collective-permute-start = (f32[2,2,2,32,256]{4,3,2,1,0:T(8,128)}, f32[2,2,2,32,256]{4,3,2,1,0:T(8,128)S(1)}, u32[]{:S(2)}, u32[]{:S(2)}) collective-permute-start(f32[2,2,2,32,256]{4,3,2,1,0:T(8,128)} %get-tuple-element.16), channel_id=1, source_target_pairs={{0,1},{1,0},{2,3},{3,2},{4,5},{5,4},{6,7},{7,6},{8,9},{9,8},{10,11... | collective-permute-start | bytes 786440 | tf_op jit(solution)/shard_map/ppermute | solution.py:421
  49.8 7.8 %collective-permute-start.1 = (f32[2,2,2,32,256]{4,3,2,1,0:T(8,128)}, f32[2,2,2,32,256]{4,3,2,1,0:T(8,128)S(1)}, u32[]{:S(2)}, u32[]{:S(2)}) collective-permute-start(f32[2,2,2,32,256]{4,3,2,1,0:T(8,128)} %get-tuple-element.17), channel_id=1, source_target_pairs={{0,2},{1,3},{2,0},{3,1},{4,6},{5,7},{6,4},{7,5},{8,10},{9,11},{10,... | collective-permute-start | bytes 786440 | tf_op jit(solution)/shard_map/ppermute | solution.py:421
  49.8 8.9 %collective-permute-start.2 = (f32[2,2,2,32,256]{4,3,2,1,0:T(8,128)}, f32[2,2,2,32,256]{4,3,2,1,0:T(8,128)S(1)}, u32[]{:S(2)}, u32[]{:S(2)}) collective-permute-start(f32[2,2,2,32,256]{4,3,2,1,0:T(8,128)} %get-tuple-element.18), channel_id=1, source_target_pairs={{0,3},{1,2},{2,1},{3,0},{4,7},{5,6},{6,5},{7,4},{8,11},{9,10},{10,... | collective-permute-start | bytes 786440 | tf_op jit(solution)/shard_map/ppermute | solution.py:421
  51.3 1.1 copy-start
  56.0 6.5 %copy-start.5 = (f32[256,256]{1,0:T(8,128)S(1)}, f32[256,256]{1,0:T(8,128)}, u32[]{:S(2)}) copy-start(f32[256,256]{1,0:T(8,128)} %get-tuple-element.24) | copy-start | bytes 786436
  56.0 9.7 %copy-start.1 = (f32[256,256]{1,0:T(8,128)S(1)}, f32[256,256]{1,0:T(8,128)}, u32[]{:S(2)}) copy-start(f32[256,256]{1,0:T(8,128)} %get-tuple-element.20.refs_4_) | copy-start | bytes 786436
  57.6 1.1 copy-start.2
  57.6 1.1 copy-start.3
  58.7 0.7 copy-start.4
  62.5 29.1 %collective-permute-start.3 = (f32[4,2,32,1024]{3,2,1,0:T(8,128)}, f32[4,2,32,1024]{3,2,1,0:T(8,128)S(1)}, u32[]{:S(2)}, u32[]{:S(2)}) collective-permute-start(f32[4,2,32,1024]{3,2,1,0:T(8,128)} %get-tuple-element.22), channel_id=1, source_target_pairs={{0,8},{1,9},{2,10},{3,11},{4,12},{5,13},{6,14},{7,15},{8,0},{9,1},... | collective-permute-start | bytes 3145736 | tf_op jit(solution)/shard_map/ppermute | solution.py:421
  62.5 3.2 %collective-permute-start.8 = (f32[256,256]{1,0:T(8,128)S(1)}, f32[256,256]{1,0:T(8,128)S(1)}, u32[]{:S(2)}, u32[]{:S(2)}) collective-permute-start(f32[256,256]{1,0:T(8,128)S(1)} %copy-done.5), channel_id=1, source_target_pairs={{0,8},{1,9},{2,10},{3,11},{4,12},{5,13},{6,14},{7,15},{8,0},{9,1},... | collective-permute-start | bytes 786440 | tf_op jit(solution)/shard_map/ppermute | solution.py:421
  66.5 20.8 %all-to-all-start.1 = ((f32[16,16,256]{2,1,0:T(8,128)}), f32[16,16,256]{2,1,0:T(8,128)S(1)}, u32[]{:S(2)}, u32[]{:S(2)}) async-start(f32[16,16,256]{2,1,0:T(8,128)} %bitcast.15), calls=%async_computation.1 | async-start | bytes 524288 | tf_op jit(solution)/shard_map/all_to_all | solution.py:457
  88.0 22.0 %all-to-all-start.2 = ((f32[16,16,256]{2,1,0:T(8,128)}), f32[16,16,256]{2,1,0:T(8,128)S(1)}, u32[]{:S(2)}, u32[]{:S(2)}) async-start(f32[16,16,256]{2,1,0:T(8,128)} %broadcast_in_dim.15), calls=%async_computation.2 | async-start | bytes 524288 | tf_op jit(solution)/shard_map/all_to_all | solution.py:462
  91.7 9.4 %collective-permute-start.4 = (f32[2,32,1024]{2,1,0:T(8,128)S(1)}, f32[2,32,1024]{2,1,0:T(8,128)S(1)}, u32[]{:S(2)}, u32[]{:S(2)}) collective-permute-start(f32[2,32,1024]{2,1,0:T(8,128)S(1)} %get-tuple-element.32), channel_id=1, source_target_pairs={{0,16},{1,17},{2,18},{3,19},{4,20},{5,21},{6,22},{7,23},{8,24},{9,... | collective-permute-start | bytes 786440 | tf_op jit(solution)/shard_map/ppermute | solution.py:421
  93.7 21.2 %collective-permute-start.6 = (f32[2,32,1024]{2,1,0:T(8,128)S(1)}, f32[2,32,1024]{2,1,0:T(8,128)S(1)}, u32[]{:S(2)}, u32[]{:S(2)}) collective-permute-start(f32[2,32,1024]{2,1,0:T(8,128)S(1)} %get-tuple-element.26), channel_id=1, source_target_pairs={{0,4},{1,5},{2,6},{3,7},{4,0},{5,1},{6,2},{7,3},{8,12},{9,13},{10,... | collective-permute-start | bytes 786440 | tf_op jit(solution)/shard_map/ppermute | solution.py:421
  101.2 15.3 %collective-permute-start.5 = (f32[32,1024]{1,0:T(8,128)S(1)}, f32[32,1024]{1,0:T(8,128)S(1)}, u32[]{:S(2)}, u32[]{:S(2)}) collective-permute-start(f32[32,1024]{1,0:T(8,128)S(1)} %fusion.4), channel_id=1, source_target_pairs={{0,4},{1,5},{2,6},{3,7},{4,0},{5,1},{6,2},{7,3},{8,12},{9,13},{10,... | collective-permute-start | bytes 393224 | tf_op jit(solution)/shard_map/ppermute | solution.py:421
  110.0 10.6 %collective-permute-start.9 = (f32[256,256]{1,0:T(8,128)S(1)}, f32[256,256]{1,0:T(8,128)S(1)}, u32[]{:S(2)}, u32[]{:S(2)}) collective-permute-start(f32[256,256]{1,0:T(8,128)S(1)} %bitcast.73), channel_id=1, source_target_pairs={{0,8},{1,9},{2,10},{3,11},{4,12},{5,13},{6,14},{7,15},{8,0},{9,1},... | collective-permute-start | bytes 786440 | tf_op jit(solution)/shard_map/ppermute | solution.py:421
  114.9 5.0 %collective-permute-start.7 = (f32[32,1024]{1,0:T(8,128)S(1)}, f32[32,1024]{1,0:T(8,128)S(1)}, u32[]{:S(2)}, u32[]{:S(2)}) collective-permute-start(f32[32,1024]{1,0:T(8,128)S(1)} %fusion.2), channel_id=1, source_target_pairs={{0,16},{1,17},{2,18},{3,19},{4,20},{5,21},{6,22},{7,23},{8,24},{9,... | collective-permute-start | bytes 393224 | tf_op jit(solution)/shard_map/ppermute | solution.py:421
